TPU v7x, 256 devices: a whole 4x4x8 slice. The times are simulated.
256 devices in a mesh: gz: 64 (over y, z, core), rows: 4 (over x).
Axes of the slice: x: 4, y: 4, z: 8, core: 2. Of those that a mesh axis runs over, the one named last changes fastest.
Arguments:
- forces: float32 [2, 6144, 4096], P(None, 'gz', 'rows'), may hold values from -40 to 40
- start: float32 [2, 6144, 4096], P(None, 'gz', 'rows'), may hold values from -4 to 4
- spring_bits: int32 [6144, 4096], P('gz', 'rows'), may hold values from 0 to 63, as said below
- plane_stiffness: float32 [6144], P('gz'), may hold values from 0.5 to 2
- cross_weight: float32 [3, 6144], P(None, 'gz'), may hold values from 0.1 to 1
- anchors: int32 [64], replicated, may hold values from 0 to 6143
Outputs:
- solution: float32 [2, 6144, 4096], P(None, 'gz', 'rows')
- residual: float32 [2, 6144, 4096], P(None, 'gz', 'rows')
Inputs may be any that keep to these rules, and one draw needn't show every extreme that they name: `spring_bits`: bit 0: right edge present; bit 1: down edge; bit 2: diagonal edge; bit 2 + j: spring to the section j before, for j = 1 to 3. `anchors`: repeats possible.
All inputs are finite; a program needn't handle non-finite values.
Results may differ from a plain program's by a relative error of at most 0.00023.
Values sent between devices are 32-bit elements; how exact they have to be, the bound alone decides.
A program may use at most 64 MiB of HBM per device.

v0:
```python
import jax
import jax.numpy as jnp
from jax import lax
from jax.sharding import Mesh
from jax.sharding import PartitionSpec as P

GRID = 64
PRED = 3
ITERS = 2
GZ = ("gz_0", "gz_1", "gz_2")


damping = 0.05
anchor_stiffness = 20.0
transverse = 0.25


def from_everyone(shard, axis):
    copies = jnp.broadcast_to(shard, (lax.axis_size(axis), *shard.shape))
    return lax.all_to_all(copies, axis, split_axis=0, concat_axis=0, tiled=True)


def over_copies(shard, axis):
    everything = from_everyone(shard, axis)
    return jnp.sum(everything, axis=0)


def over_axes(shard, axes):
    far, near = axes
    return over_copies(over_copies(shard, near), far)


def packed_total(arrays, axis):
    flat, at, done = (jnp.concatenate([a.reshape(-1) for a in arrays]), 0, [])
    total = over_axes(flat, axis)
    for a in arrays:
        done.append(total[at : at + a.size].reshape(a.shape))
        at += a.size
    return tuple(done)


def from_behind(value, axis, steps):
    count = lax.axis_size(axis)
    first, last = (max(0, -steps), min(count, count - steps))
    return lax.ppermute(value, axis, [(source, source + steps) for source in range(first, last)])


def extended(shard, sides, width):
    for axis, dim in sides:
        size, length = (lax.axis_size(axis), shard.shape[dim])
        up = [(i, (i + 1) % size) for i in range(size - 1)]
        down = [(j, i) for i, j in up]
        last = lax.slice_in_dim(shard, length - width, length, axis=dim)
        first = lax.slice_in_dim(shard, 0, width, axis=dim)
        before = lax.ppermute(last, axis, up)
        after = lax.ppermute(first, axis, down)
        shard = jnp.concatenate([before, shard, after], axis=dim)
    return shard


def bit_plane(spring_bits, bit_index):
    return (spring_bits // 2**bit_index % 2).astype(jnp.float32)


def edge_pull(edge_kind, weight, stretch):
    first_part = stretch[0]
    second_part = stretch[1]
    if edge_kind == "right":
        return jnp.stack([weight * first_part, weight * transverse * second_part])
    if edge_kind == "down":
        return jnp.stack([weight * transverse * first_part, weight * second_part])
    halved = 0.5 * weight
    return jnp.stack(
        [
            halved * ((1.0 + transverse) * first_part + (1.0 - transverse) * second_part),
            halved * ((1.0 - transverse) * first_part + (1.0 + transverse) * second_part),
        ]
    )


def paired(residual, precond, mapped):
    return packed_total(
        (jnp.sum(residual * precond), jnp.sum(mapped * precond)),
        (("gz_0", "gz_1"), ("gz_2", "rows")),
    )


def per_device(forces, start, spring_bits, plane_stiffness, cross_weight, anchors):
    sections = forces.shape[1]
    strip = forces.shape[2]
    node_index = jnp.arange(strip, dtype=jnp.int32)
    column = (node_index % GRID)[None, :]
    grid_row = (lax.axis_index("rows") * (strip // GRID) + node_index // GRID)[None, :]
    section_index = lax.axis_index(GZ) * sections + jnp.arange(sections, dtype=jnp.int32)
    stiffness = plane_stiffness[:, None]
    open_column = (column < GRID - 1).astype(jnp.float32)
    open_row = (grid_row < GRID - 1).astype(jnp.float32)
    w_right = stiffness * bit_plane(spring_bits, 0) * open_column
    w_down = stiffness * bit_plane(spring_bits, 1) * open_row
    w_diag = stiffness * bit_plane(spring_bits, 2) * open_column * open_row
    w_cross = jnp.stack(
        [
            cross_weight[lag_index][:, None]
            * bit_plane(spring_bits, 3 + lag_index)
            * (section_index > lag_index).astype(jnp.float32)[:, None]
            for lag_index in range(PRED)
        ]
    )
    upper_rims = from_behind(
        jnp.stack([w_down[:, strip - GRID :], w_diag[:, strip - GRID :]]), "rows", 1
    )
    later_cross = from_behind(w_cross[:, :PRED, :], GZ, -1)
    cross_ext = jnp.concatenate([w_cross, later_cross], axis=1)
    down_ext = jnp.concatenate([upper_rims[0], w_down], axis=1)
    diag_ext = jnp.concatenate([upper_rims[1], w_diag], axis=1)
    anchored = jnp.any(anchors[None, :] == section_index[:, None], axis=1).astype(jnp.float32)
    tethers = (damping + anchor_stiffness * anchored)[:, None]
    right_in = jnp.pad(w_right[:, :-1], ((0, 0), (1, 0)))
    down_in = down_ext[:, :strip]
    diag_in = jnp.pad(diag_ext[:, : strip - 1], ((0, 0), (1, 0)))
    cross_sum = jnp.zeros_like(w_right)
    for lag_index in range(PRED):
        offset = lag_index + 1
        cross_sum = (
            cross_sum + w_cross[lag_index] + cross_ext[lag_index, offset : offset + sections]
        )
    shared = tethers + 0.5 * (1.0 + transverse) * (w_diag + diag_in) + cross_sum
    diag_first = shared + (w_right + right_in) + transverse * (w_down + down_in)
    diag_second = shared + transverse * (w_right + right_in) + (w_down + down_in)
    inverse = 1.0 / jnp.stack([diag_first, diag_second])

    def operate(vector):
        planes = extended(vector, ((GZ, 1),), PRED)
        balance = tethers[None] * vector
        owners = planes[:, PRED:]
        for lag_index in range(PRED):
            offset = lag_index + 1
            partner = planes[:, PRED - offset : PRED - offset + sections + PRED]
            tension = cross_ext[lag_index][None] * (owners - partner)
            balance = balance + tension[:, :sections] - tension[:, offset : offset + sections]
        beside = jnp.pad(vector[:, :, 1:], ((0, 0), (0, 0), (0, 1)))
        tension = edge_pull("right", w_right, vector - beside)
        balance = balance + tension - jnp.pad(tension[:, :, :-1], ((0, 0), (0, 0), (1, 0)))
        padded = extended(vector, (("rows", 2),), GRID)
        top_owners = padded[:, :, : strip + GRID]
        beneath = padded[:, :, GRID:]
        corners = jnp.pad(padded[:, :, GRID + 1 :], ((0, 0), (0, 0), (0, 1)))
        pull_down = edge_pull("down", down_ext, top_owners - beneath)
        pull_diag = edge_pull("diag", diag_ext, top_owners - corners)
        balance = balance + pull_down[:, :, GRID:] - pull_down[:, :, :strip]
        balance = (
            balance
            + pull_diag[:, :, GRID:]
            - jnp.pad(pull_diag[:, :, : strip - 1], ((0, 0), (0, 0), (1, 0)))
        )
        return balance

    solution = start
    residual = forces - operate(solution)
    precond = residual * inverse
    mapped = operate(precond)
    inner_now, curvature = paired(residual, precond, mapped)
    step_size = inner_now / curvature
    direction = precond
    mapped_dir = mapped
    for iteration in range(ITERS):
        solution = solution + step_size * direction
        if iteration + 1 < ITERS:
            residual = residual - step_size * mapped_dir
            precond = residual * inverse
            mapped = operate(precond)
            inner_next, curvature = paired(residual, precond, mapped)
            growth = inner_next / inner_now
            step_size = inner_next / (curvature - growth * inner_next / step_size)
            direction = precond + growth * direction
            mapped_dir = mapped + growth * mapped_dir
            inner_now = inner_next
        else:
            residual = residual - step_size * mapped_dir
    return (solution, residual)


def solution(mesh):
    finer = Mesh(
        mesh.devices.reshape(4, 8, 2, mesh.shape["rows"]), ("gz_0", "gz_1", "gz_2", "rows")
    )
    return jax.shard_map(
        per_device,
        mesh=finer,
        in_specs=(P(None, GZ, "rows"), P(None, GZ, "rows"), P(GZ, "rows"), P(GZ), P(None, GZ), P()),
        out_specs=(P(None, GZ, "rows"), P(None, GZ, "rows")),
        check_vma=False,
    )
```

profile of v0, /device:TPU:1, one launch (start us, length us, event | category | flops | bytes accessed | tf_op | source)
XLA Modules:
  0.0 137.8 jit_solution(9845884385524787205)
XLA Ops:
  0.7 1.0 fusion.121
  1.6 4.9 %collective-permute-start.2 = (f32[2,3,1024]{2,1,0:T(4,128)S(1)}, f32[2,3,1024]{2,1,0:T(4,128)S(1)}, u32[]{:S(2)}, u32[]{:S(2)}) collective-permute-start(f32[2,3,1024]{2,1,0:T(4,128)S(1)} %get-tuple-element.56), channel_id=1, source_target_pairs={{0,4},{4,8},{8,12},{12,16},{16,20},{20,24},{24,28},{28,32},{32,36}... | collective-permute-start | bytes 73736 | tf_op jit(solution)/shard_map/ppermute | solution.py:55
  6.5 1.9 %collective-permute-start.1 = (f32[2,3,1024]{2,1,0:T(4,128)S(1)}, f32[2,3,1024]{2,1,0:T(4,128)S(1)}, u32[]{:S(2)}, u32[]{:S(2)}) collective-permute-start(f32[2,3,1024]{2,1,0:T(4,128)S(1)} %get-tuple-element.57), channel_id=1, source_target_pairs={{4,0},{8,4},{12,8},{16,12},{20,16},{24,20},{28,24},{32,28},{36,32}... | collective-permute-start | bytes 73736 | tf_op jit(solution)/shard_map/ppermute | solution.py:56
  8.5 1.0 fusion.122
  9.5 3.1 %collective-permute-start.4 = (f32[2,96,64]{2,1,0:T(8,128)S(1)}, f32[2,96,64]{2,1,0:T(8,128)S(1)}, u32[]{:S(2)}, u32[]{:S(2)}) collective-permute-start(f32[2,96,64]{2,1,0:T(8,128)S(1)} %get-tuple-element.61), channel_id=1, source_target_pairs={{0,1},{1,2},{2,3},{4,5},{5,6},{6,7},{8,9},{9,10},{10,11},{12,13},{... | collective-permute-start | bytes 147464 | tf_op jit(solution)/shard_map/ppermute | solution.py:55
  12.6 1.3 collective-permute-start.5
  14.0 1.4 %slice.338 = f32[2,96,1023]{2,1,0:T(8,128)S(1)} slice(f32[2,96,1024]{2,1,0:T(8,128)} %param.7), slice={[0:2], [0:96], [1:1024]} | slice | bytes 1571328 | tf_op jit(solution)/shard_map/slice | solution.py:141
  15.5 0.2 constant_dynamic-update-slice_fusion.1
  15.7 0.7 copy-done.16
  16.4 1.9 %fusion.111 = (f32[1,96,1024]{2,1,0:T(8,128)S(1)}, f32[1,96,1024]{2,1,0:T(8,128)S(1)}, f32[1,96,1024]{2,1,0:T(8,128)S(1)}, f32[96,1024]{1,0:T(8,128)S(1)}, f32[9...) fusion(f32[96]{0:T(128)S(1)} %compare_convert_fusion.2, s32[96,1024]{1,0:T(8,128)S(1)} %copy-done.16, ...), kind=kLoop, calls=%fused_computation.285 | loop fusion | flops 13172736 | bytes 3549824 | tf_op jit(solution)/shard_map/stack | solution.py:101
  18.4 1.9 %collective-permute-start = (f32[3,3,1024]{2,1,0:T(4,128)S(1)}, f32[3,3,1024]{2,1,0:T(4,128)S(1)}, u32[]{:S(2)}, u32[]{:S(2)}) collective-permute-start(f32[3,3,1024]{2,1,0:T(4,128)S(1)} %pad_maximum_fusion.20), channel_id=1, source_target_pairs={{4,0},{8,4},{12,8},{16,12},{20,16},{24,20},{28,24},{32,28},{36,32}... | collective-permute-start | bytes 110600 | tf_op jit(solution)/shard_map/ppermute | solution.py:45
  20.6 4.0 %collective-permute-start.3 = (f32[2,96,64]{2,1,0:T(8,128)S(1)}, f32[2,96,64]{2,1,0:T(8,128)S(1)}, u32[]{:S(2)}, u32[]{:S(2)}) collective-permute-start(f32[2,96,64]{2,1,0:T(8,128)S(1)} %pad_maximum_fusion.19), channel_id=1, source_target_pairs={{0,1},{1,2},{2,3},{4,5},{5,6},{6,7},{8,9},{9,10},{10,11},{12,13},{... | collective-permute-start | bytes 147464 | tf_op jit(solution)/shard_map/ppermute | solution.py:45
  25.1 0.5 fusion.9
  25.5 0.7 collective-permute-done.3
  26.3 1.5 %add_bitcast_fusion.1 = (f32[1,96,1024]{2,1,0:T(8,128)S(1)}, f32[96,1024]{1,0:T(8,128)S(1)}) fusion(f32[96,1024]{1,0:T(8,128)S(1)} %get-tuple-element.70, f32[96,64]{1,0:T(8,128)S(1)} %get-tuple-element.75, f32[96,1024]{1,0:T(8,128)S(1)} %get-tuple-element.73, f32[96,1023]{1,0:T(8,128)S(1)} %bitcast.114, f32[3,99,1024]{2,1,0:T(8,128)S(1)} %pad_maximum_fusion, ...), kind=kLoop, calls=%fused_computation.236 | loop fusion | flops 9437184 | bytes 3983616 | tf_op jit(solution)/shard_map/stack | solution.py:130
  27.8 0.3 fusion.89
  28.2 0.3 slice.440
  28.5 0.3 fusion.41
  28.8 0.2 slice_multiply_fusion.5
  29.0 0.2 add_multiply_fusion.5
  29.3 0.9 copy-done.17
  30.2 1.1 fusion.98
  31.4 0.3 slice.459
  31.7 1.9 %collective-permute-start.6 = (f32[2,3,1024]{2,1,0:T(4,128)S(1)}, f32[2,3,1024]{2,1,0:T(4,128)S(1)}, u32[]{:S(2)}, u32[]{:S(2)}) collective-permute-start(f32[2,3,1024]{2,1,0:T(4,128)S(1)} %get-tuple-element.52), channel_id=1, source_target_pairs={{4,0},{8,4},{12,8},{16,12},{20,16},{24,20},{28,24},{32,28},{36,32}... | collective-permute-start | bytes 73736 | tf_op jit(solution)/shard_map/ppermute | solution.py:56
  33.6 5.6 %collective-permute-start.7 = (f32[2,3,1024]{2,1,0:T(4,128)S(1)}, f32[2,3,1024]{2,1,0:T(4,128)S(1)}, u32[]{:S(2)}, u32[]{:S(2)}) collective-permute-start(f32[2,3,1024]{2,1,0:T(4,128)S(1)} %get-tuple-element.53), channel_id=1, source_target_pairs={{0,4},{4,8},{8,12},{12,16},{16,20},{20,24},{24,28},{28,32},{32,36}... | collective-permute-start | bytes 73736 | tf_op jit(solution)/shard_map/ppermute | solution.py:55
  39.1 4.1 %collective-permute-start.8 = (f32[2,96,64]{2,1,0:T(8,128)S(1)}, f32[2,96,64]{2,1,0:T(8,128)S(1)}, u32[]{:S(2)}, u32[]{:S(2)}) collective-permute-start(f32[2,96,64]{2,1,0:T(8,128)S(1)} %get-tuple-element.54), channel_id=1, source_target_pairs={{0,1},{1,2},{2,3},{4,5},{5,6},{6,7},{8,9},{9,10},{10,11},{12,13},{... | collective-permute-start | bytes 147464 | tf_op jit(solution)/shard_map/ppermute | solution.py:55
  43.3 1.3 collective-permute-start.9
  45.0 0.4 fusion.7
  45.4 3.2 %collective-permute-done.9 = f32[2,96,64]{2,1,0:T(8,128)S(1)} collective-permute-done((f32[2,96,64]{2,1,0:T(8,128)S(1)}, f32[2,96,64]{2,1,0:T(8,128)S(1)}, u32[]{:S(2)}, u32[]{:S(2)}) %collective-permute-start.9) | collective-permute-done | bytes 49184 | tf_op jit(solution)/shard_map/ppermute | solution.py:56
  48.6 0.3 fusion.3
  49.0 0.3 fusion.2
  49.3 0.2 slice_multiply_fusion.3
  49.5 0.2 add_multiply_fusion.3
  49.7 2.6 %multiply_reduce_fusion.3 = (f32[]{:T(128)}, f32[]{:T(128)}, f32[2,96,1024]{2,1,0:T(8,128)}) fusion(f32[2,96,1024]{2,1,0:T(8,128)S(1)} %get-tuple-element.9, f32[2,96,1024]{2,1,0:T(8,128)S(1)} %get-tuple-element.8, f32[1,96,1088]{2,1,0:T(8,128)S(1)} %get-tuple-element.27, f32[1,96,1088]{2,1,0:T(8,128)S(1)} %get-tuple-element.26, ...), kind=kLoop, calls=%fused_computation.121 | loop fusion | flops 4915198 | bytes 10321544 | tf_op jit(solution)/shard_map/reduce_sum | solution.py:83
  52.4 1.3 pad_maximum_fusion.22
  53.7 8.5 %all_to_all.24 = f32[8,1,2]{2,1,0:T(1,128)S(1)} all-to-all(f32[8,1,2]{2,1,0:T(1,128)S(1)} %broadcast_in_dim.8), channel_id=1, replica_groups=mesh['gz_0'=4,'gz_1'=8,'gz_2'=2,'rows'=4] {'gz_2','rows'}, dimensions={0} | all-to-all | bytes 128 | tf_op jit(solution)/shard_map/all_to_all | solution.py:20
  62.2 21.9 %all_to_all.25 = f32[32,1,2]{2,1,0:T(1,128)S(1)} all-to-all(f32[32,1,2]{2,1,0:T(1,128)S(1)} %broadcast_in_dim.9), channel_id=1, replica_groups=mesh['gz_0'=4,'gz_1'=8,'gz_2'=2,'rows'=4] {'gz_0','gz_1'}, dimensions={0} | all-to-all | bytes 512 | tf_op jit(solution)/shard_map/all_to_all | solution.py:20
  84.1 0.6 fusion.125
  86.1 1.6 %fusion.97 = f32[2,96,1024]{2,1,0:T(8,128)S(1)} fusion(f32[2,96,1024]{2,1,0:T(8,128)S(1)} %get-tuple-element.9, f32[2,96,1024]{2,1,0:T(8,128)} %get-tuple-element.7, f32[]{:T(128)S(6)} %div.98, f32[1,96,1024]{2,1,0:T(8,128)} %copy-done.14, f32[1,96,1024]{2,1,0:T(8,128)} %copy-done.13), kind=kLoop, calls=%fused_computation.244 | loop fusion | flops 983040 | bytes 3145732 | tf_op jit(solution)/shard_map/mul | solution.py:170
  87.7 0.3 slice.486
  88.0 4.0 %collective-permute-start.10 = (f32[2,3,1024]{2,1,0:T(4,128)S(1)}, f32[2,3,1024]{2,1,0:T(4,128)S(1)}, u32[]{:S(2)}, u32[]{:S(2)}) collective-permute-start(f32[2,3,1024]{2,1,0:T(4,128)S(1)} %get-tuple-element.48), channel_id=1, source_target_pairs={{4,0},{8,4},{12,8},{16,12},{20,16},{24,20},{28,24},{32,28},{36,32}... | collective-permute-start | bytes 73736 | tf_op jit(solution)/shard_map/ppermute | solution.py:56
  92.0 2.2 %collective-permute-start.11 = (f32[2,3,1024]{2,1,0:T(4,128)S(1)}, f32[2,3,1024]{2,1,0:T(4,128)S(1)}, u32[]{:S(2)}, u32[]{:S(2)}) collective-permute-start(f32[2,3,1024]{2,1,0:T(4,128)S(1)} %get-tuple-element.49), channel_id=1, source_target_pairs={{0,4},{4,8},{8,12},{12,16},{16,20},{20,24},{24,28},{28,32},{32,36}... | collective-permute-start | bytes 73736 | tf_op jit(solution)/shard_map/ppermute | solution.py:55
  94.2 2.2 %collective-permute-start.12 = (f32[2,96,64]{2,1,0:T(8,128)S(1)}, f32[2,96,64]{2,1,0:T(8,128)S(1)}, u32[]{:S(2)}, u32[]{:S(2)}) collective-permute-start(f32[2,96,64]{2,1,0:T(8,128)S(1)} %get-tuple-element.50), channel_id=1, source_target_pairs={{0,1},{1,2},{2,3},{4,5},{5,6},{6,7},{8,9},{9,10},{10,11},{12,13},{... | collective-permute-start | bytes 147464 | tf_op jit(solution)/shard_map/ppermute | solution.py:55
  96.4 1.3 collective-permute-start.13
  98.1 0.8 copy-done.8
  98.9 0.1 copy-done.10
  99.1 0.1 copy-done.12
  99.2 0.5 fusion.5
  99.7 2.4 %collective-permute-done.13 = f32[2,96,64]{2,1,0:T(8,128)S(1)} collective-permute-done((f32[2,96,64]{2,1,0:T(8,128)S(1)}, f32[2,96,64]{2,1,0:T(8,128)S(1)}, u32[]{:S(2)}, u32[]{:S(2)}) %collective-permute-start.13) | collective-permute-done | bytes 49184 | tf_op jit(solution)/shard_map/ppermute | solution.py:56
  102.1 0.3 fusion.1
  102.5 0.3 fusion
  102.8 0.6 copy-done.2
  103.4 0.2 slice_multiply_fusion.1
  103.6 0.2 copy-done.6
  103.8 0.2 add_multiply_fusion.1
  104.0 0.8 copy-done.3
  104.8 2.5 %multiply_reduce_fusion.1 = (f32[]{:T(128)}, f32[]{:T(128)}, f32[2,96,1024]{2,1,0:T(8,128)}) fusion(f32[2,96,1024]{2,1,0:T(8,128)S(1)} %fusion.97, f32[2,96,1024]{2,1,0:T(8,128)S(1)} %get-tuple-element.9, f32[2,96,1024]{2,1,0:T(8,128)S(1)} %copy-done.3, f32[]{:T(128)S(6)} %div.98, f32[1,96,1088]{2,1,0:T(8,128)S(1)} %get-tuple-element.23, ...), kind=kLoop, calls=%fused_computation.117 | loop fusion | flops 5308414 | bytes 11107980 | tf_op jit(solution)/shard_map/reduce_sum | solution.py:83
  107.3 1.3 pad_maximum_fusion.23
  108.6 9.1 %all_to_all.26 = f32[8,1,2]{2,1,0:T(1,128)S(1)} all-to-all(f32[8,1,2]{2,1,0:T(1,128)S(1)} %broadcast_in_dim.10), channel_id=1, replica_groups=mesh['gz_0'=4,'gz_1'=8,'gz_2'=2,'rows'=4] {'gz_2','rows'}, dimensions={0} | all-to-all | bytes 128 | tf_op jit(solution)/shard_map/all_to_all | solution.py:20
  117.8 12.3 %all_to_all.27 = f32[32,1,2]{2,1,0:T(1,128)S(1)} all-to-all(f32[32,1,2]{2,1,0:T(1,128)S(1)} %broadcast_in_dim.11), channel_id=1, replica_groups=mesh['gz_0'=4,'gz_1'=8,'gz_2'=2,'rows'=4] {'gz_0','gz_1'}, dimensions={0} | all-to-all | bytes 512 | tf_op jit(solution)/shard_map/all_to_all | solution.py:20
  130.2 0.6 fusion.124
  135.1 1.1 multiply_add_fusion
  136.2 0.5 copy-done.15
  136.7 1.1 multiply_subtract_fusion
  (90 shorter events, 2.0 us)
Async XLA Ops:
  0.6 14.8 %copy-start = (f32[2,96,1024]{2,1,0:T(8,128)S(1)}, f32[2,96,1024]{2,1,0:T(8,128)}, u32[]{:S(2)}) copy-start(f32[2,96,1024]{2,1,0:T(8,128)} %param.7) | copy-start | bytes 2359300
  0.6 14.7 %copy-start.22 = (f32[3,96]{1,0:T(4,128)S(1)}, f32[3,96]{1,0:T(4,128)}, u32[]{:S(2)}) copy-start(f32[3,96]{1,0:T(4,128)} %param.10) | copy-start | bytes 3460
  1.6 19.0 %collective-permute-start.2 = (f32[2,3,1024]{2,1,0:T(4,128)S(1)}, f32[2,3,1024]{2,1,0:T(4,128)S(1)}, u32[]{:S(2)}, u32[]{:S(2)}) collective-permute-start(f32[2,3,1024]{2,1,0:T(4,128)S(1)} %get-tuple-element.56), channel_id=1, source_target_pairs={{0,4},{4,8},{8,12},{12,16},{16,20},{20,24},{24,28},{28,32},{32,36}... | collective-permute-start | bytes 73736 | tf_op jit(solution)/shard_map/ppermute | solution.py:55
  6.5 18.1 %collective-permute-start.1 = (f32[2,3,1024]{2,1,0:T(4,128)S(1)}, f32[2,3,1024]{2,1,0:T(4,128)S(1)}, u32[]{:S(2)}, u32[]{:S(2)}) collective-permute-start(f32[2,3,1024]{2,1,0:T(4,128)S(1)} %get-tuple-element.57), channel_id=1, source_target_pairs={{4,0},{8,4},{12,8},{16,12},{20,16},{24,20},{28,24},{32,28},{36,32}... | collective-permute-start | bytes 73736 | tf_op jit(solution)/shard_map/ppermute | solution.py:56
  9.5 19.0 %collective-permute-start.4 = (f32[2,96,64]{2,1,0:T(8,128)S(1)}, f32[2,96,64]{2,1,0:T(8,128)S(1)}, u32[]{:S(2)}, u32[]{:S(2)}) collective-permute-start(f32[2,96,64]{2,1,0:T(8,128)S(1)} %get-tuple-element.61), channel_id=1, source_target_pairs={{0,1},{1,2},{2,3},{4,5},{5,6},{6,7},{8,9},{9,10},{10,11},{12,13},{... | collective-permute-start | bytes 147464 | tf_op jit(solution)/shard_map/ppermute | solution.py:55
  12.6 15.5 %collective-permute-start.5 = (f32[2,96,64]{2,1,0:T(8,128)S(1)}, f32[2,96,64]{2,1,0:T(8,128)S(1)}, u32[]{:S(2)}, u32[]{:S(2)}) collective-permute-start(f32[2,96,64]{2,1,0:T(8,128)S(1)} %get-tuple-element.62), channel_id=1, source_target_pairs={{1,0},{2,1},{3,2},{5,4},{6,5},{7,6},{9,8},{10,9},{11,10},{13,12},{... | collective-permute-start | bytes 147464 | tf_op jit(solution)/shard_map/ppermute | solution.py:56
  15.4 1.0 copy-start.16
  15.4 1.0 copy-start.23
  16.4 3.9 %copy-start.24 = (s32[64]{0:T(128)S(1)}, s32[64]{0:T(128)}, u32[]{:S(2)}) copy-start(s32[64]{0:T(128)} %param.11) | copy-start | bytes 772
  18.4 30.9 %copy-start.1 = (f32[96,1024]{1,0:T(8,128)}, f32[96,1024]{1,0:T(8,128)S(1)}, u32[]{:S(2)}) copy-start(f32[96,1024]{1,0:T(8,128)S(1)} %get-tuple-element.70) | copy-start | bytes 1179652
  18.4 31.1 %copy-start.5 = (f32[96,1024]{1,0:T(8,128)}, f32[96,1024]{1,0:T(8,128)S(1)}, u32[]{:S(2)}) copy-start(f32[96,1024]{1,0:T(8,128)S(1)} %get-tuple-element.71) | copy-start | bytes 1179652
  18.4 6.4 %collective-permute-start = (f32[3,3,1024]{2,1,0:T(4,128)S(1)}, f32[3,3,1024]{2,1,0:T(4,128)S(1)}, u32[]{:S(2)}, u32[]{:S(2)}) collective-permute-start(f32[3,3,1024]{2,1,0:T(4,128)S(1)} %pad_maximum_fusion.20), channel_id=1, source_target_pairs={{4,0},{8,4},{12,8},{16,12},{20,16},{24,20},{28,24},{32,28},{36,32}... | collective-permute-start | bytes 110600 | tf_op jit(solution)/shard_map/ppermute | solution.py:45
  20.6 5.6 %collective-permute-start.3 = (f32[2,96,64]{2,1,0:T(8,128)S(1)}, f32[2,96,64]{2,1,0:T(8,128)S(1)}, u32[]{:S(2)}, u32[]{:S(2)}) collective-permute-start(f32[2,96,64]{2,1,0:T(8,128)S(1)} %pad_maximum_fusion.19), channel_id=1, source_target_pairs={{0,1},{1,2},{2,3},{4,5},{5,6},{6,7},{8,9},{9,10},{10,11},{12,13},{... | collective-permute-start | bytes 147464 | tf_op jit(solution)/shard_map/ppermute | solution.py:45
  25.0 20.0 %copy-start.7 = (f32[99,1024]{1,0:T(8,128)}, f32[99,1024]{1,0:T(8,128)S(1)}, u32[]{:S(2)}) copy-start(f32[99,1024]{1,0:T(8,128)S(1)} %get-tuple-element.32) | copy-start | bytes 1216516
  25.0 20.0 %copy-start.9 = (f32[99,1024]{1,0:T(8,128)}, f32[99,1024]{1,0:T(8,128)S(1)}, u32[]{:S(2)}) copy-start(f32[99,1024]{1,0:T(8,128)S(1)} %get-tuple-element.33) | copy-start | bytes 1216516
  25.0 20.0 %copy-start.11 = (f32[99,1024]{1,0:T(8,128)}, f32[99,1024]{1,0:T(8,128)S(1)}, u32[]{:S(2)}) copy-start(f32[99,1024]{1,0:T(8,128)S(1)} %get-tuple-element.34) | copy-start | bytes 1216516
  26.3 23.0 %copy-start.20 = (f32[1,96,64]{2,1,0:T(8,128)}, f32[1,96,64]{2,1,0:T(8,128)S(1)}, u32[]{:S(2)}) copy-start(f32[1,96,64]{2,1,0:T(8,128)S(1)} %get-tuple-element.74) | copy-start | bytes 73732
  26.3 23.2 %copy-start.18 = (f32[1,96,64]{2,1,0:T(8,128)}, f32[1,96,64]{2,1,0:T(8,128)S(1)}, u32[]{:S(2)}) copy-start(f32[1,96,64]{2,1,0:T(8,128)S(1)} %get-tuple-element.77) | copy-start | bytes 73732
  27.8 1.5 %copy-start.13 = (f32[1,96,1024]{2,1,0:T(8,128)}, f32[1,96,1024]{2,1,0:T(8,128)S(1)}, u32[]{:S(2)}) copy-start(f32[1,96,1024]{2,1,0:T(8,128)S(1)} %get-tuple-element.10) | copy-start | bytes 1179652
  28.1 1.2 copy-start.14
  29.0 1.1 copy-start.17
  31.7 13.2 %collective-permute-start.6 = (f32[2,3,1024]{2,1,0:T(4,128)S(1)}, f32[2,3,1024]{2,1,0:T(4,128)S(1)}, u32[]{:S(2)}, u32[]{:S(2)}) collective-permute-start(f32[2,3,1024]{2,1,0:T(4,128)S(1)} %get-tuple-element.52), channel_id=1, source_target_pairs={{4,0},{8,4},{12,8},{16,12},{20,16},{24,20},{28,24},{32,28},{36,32}... | collective-permute-start | bytes 73736 | tf_op jit(solution)/shard_map/ppermute | solution.py:56
  33.6 11.3 %collective-permute-start.7 = (f32[2,3,1024]{2,1,0:T(4,128)S(1)}, f32[2,3,1024]{2,1,0:T(4,128)S(1)}, u32[]{:S(2)}, u32[]{:S(2)}) collective-permute-start(f32[2,3,1024]{2,1,0:T(4,128)S(1)} %get-tuple-element.53), channel_id=1, source_target_pairs={{0,4},{4,8},{8,12},{12,16},{16,20},{20,24},{24,28},{28,32},{32,36}... | collective-permute-start | bytes 73736 | tf_op jit(solution)/shard_map/ppermute | solution.py:55
  39.1 9.8 %collective-permute-start.8 = (f32[2,96,64]{2,1,0:T(8,128)S(1)}, f32[2,96,64]{2,1,0:T(8,128)S(1)}, u32[]{:S(2)}, u32[]{:S(2)}) collective-permute-start(f32[2,96,64]{2,1,0:T(8,128)S(1)} %get-tuple-element.54), channel_id=1, source_target_pairs={{0,1},{1,2},{2,3},{4,5},{5,6},{6,7},{8,9},{9,10},{10,11},{12,13},{... | collective-permute-start | bytes 147464 | tf_op jit(solution)/shard_map/ppermute | solution.py:55
  43.3 5.4 %collective-permute-start.9 = (f32[2,96,64]{2,1,0:T(8,128)S(1)}, f32[2,96,64]{2,1,0:T(8,128)S(1)}, u32[]{:S(2)}, u32[]{:S(2)}) collective-permute-start(f32[2,96,64]{2,1,0:T(8,128)S(1)} %get-tuple-element.55), channel_id=1, source_target_pairs={{1,0},{2,1},{3,2},{5,4},{6,5},{7,6},{9,8},{10,9},{11,10},{13,12},{... | collective-permute-start | bytes 147464 | tf_op jit(solution)/shard_map/ppermute | solution.py:56
  88.0 10.0 %collective-permute-start.10 = (f32[2,3,1024]{2,1,0:T(4,128)S(1)}, f32[2,3,1024]{2,1,0:T(4,128)S(1)}, u32[]{:S(2)}, u32[]{:S(2)}) collective-permute-start(f32[2,3,1024]{2,1,0:T(4,128)S(1)} %get-tuple-element.48), channel_id=1, source_target_pairs={{4,0},{8,4},{12,8},{16,12},{20,16},{24,20},{28,24},{32,28},{36,32}... | collective-permute-start | bytes 73736 | tf_op jit(solution)/shard_map/ppermute | solution.py:56
  92.0 6.0 %collective-permute-start.11 = (f32[2,3,1024]{2,1,0:T(4,128)S(1)}, f32[2,3,1024]{2,1,0:T(4,128)S(1)}, u32[]{:S(2)}, u32[]{:S(2)}) collective-permute-start(f32[2,3,1024]{2,1,0:T(4,128)S(1)} %get-tuple-element.49), channel_id=1, source_target_pairs={{0,4},{4,8},{8,12},{12,16},{16,20},{20,24},{24,28},{28,32},{32,36}... | collective-permute-start | bytes 73736 | tf_op jit(solution)/shard_map/ppermute | solution.py:55
  94.2 8.3 %collective-permute-start.12 = (f32[2,96,64]{2,1,0:T(8,128)S(1)}, f32[2,96,64]{2,1,0:T(8,128)S(1)}, u32[]{:S(2)}, u32[]{:S(2)}) collective-permute-start(f32[2,96,64]{2,1,0:T(8,128)S(1)} %get-tuple-element.50), channel_id=1, source_target_pairs={{0,1},{1,2},{2,3},{4,5},{5,6},{6,7},{8,9},{9,10},{10,11},{12,13},{... | collective-permute-start | bytes 147464 | tf_op jit(solution)/shard_map/ppermute | solution.py:55
  96.4 5.7 %collective-permute-start.13 = (f32[2,96,64]{2,1,0:T(8,128)S(1)}, f32[2,96,64]{2,1,0:T(8,128)S(1)}, u32[]{:S(2)}, u32[]{:S(2)}) collective-permute-start(f32[2,96,64]{2,1,0:T(8,128)S(1)} %get-tuple-element.51), channel_id=1, source_target_pairs={{1,0},{2,1},{3,2},{5,4},{6,5},{7,6},{9,8},{10,9},{11,10},{13,12},{... | collective-permute-start | bytes 147464 | tf_op jit(solution)/shard_map/ppermute | solution.py:56
  97.9 1.0 copy-start.8
  97.9 1.1 copy-start.10
  97.9 1.2 copy-start.12
  102.4 1.0 copy-start.2
  102.4 1.0 copy-start.21
  102.8 1.0 copy-start.6
  102.8 1.0 copy-start.19
  103.6 1.2 copy-start.3
  135.1 1.1 copy-start.4
  135.1 1.6 %copy-start.15 = (f32[2,96,1024]{2,1,0:T(8,128)S(1)}, f32[2,96,1024]{2,1,0:T(8,128)}, u32[]{:S(2)}) copy-start(f32[2,96,1024]{2,1,0:T(8,128)} %get-tuple-element.6) | copy-start | bytes 2359300
where the time goes:
time: 139 us; the launch traced here: 138 us
  blocking collectives  51.8 us (37%)
  starting transfers between devices  39.7 us (29%)
  other arithmetic  22.1 us (16%)
  local copies, waits for them, and re-layouts  10.8 us (8%)
  between operations  7.06 us (5%)
  waiting for transfers between devices  6.36 us (5%)
    all_to_all x4, blocking collectives, from_everyone(): return lax.all_to_all(copies, axis, split_axis=0, concat_axis=0, tiled=True)  51.8 us
    ppermute x6, starting transfers between devices, extended(): before = lax.ppermute(last, axis, up)  22.1 us
    ppermute x6, starting transfers between devices, extended(): after = lax.ppermute(first, axis, down)  11.7 us
    ppermute x2, starting transfers between devices, from_behind(): lax.ppermute(value, axis, [(source, source + steps) for source in range(f...  5.91 us
    ppermute x6, waiting for transfers between devices, extended(): after = lax.ppermute(first, axis, down)  5.63 us
    reduce_sum x2, other arithmetic, paired(): jnp.sum(residual * precond)  5.17 us
    unnamed x50, local copies, waits for them, and re-layouts  4.86 us
  transfers between devices with their start and end apart: 14, of which 3 were waited for; matrix products, arithmetic and copies ran while one was open for 7% of the time, Pallas kernels for 0%

commit v1 on v0

v1 whole, which is shorter than its diff:
```python
import functools

import jax
import jax.numpy as jnp
from jax import lax
from jax.experimental import pallas as pl
from jax.experimental.pallas import tpu as pltpu
from jax.sharding import PartitionSpec as P

GRID = 64
PRED = 3
LANES = 128
MESH = pl.DeviceIdType.MESH

damping = 0.05
anchor_stiffness = 20.0


def digit_sizes(size):
    return (4, 8, 2) if size == 64 else (1, size // 2, 2)


def stage_groups(size, rows):
    ny, nz, nc = digit_sizes(size)
    near = [(0, 0, c, x) for c in range(nc) for x in range(rows)][1:]
    far = [(y, z, 0, 0) for y in range(ny) for z in range(nz)][1:]
    return [group for group in (near, far) if group]


def kernel(
    n_gz, n_rows, n_anchors, stages,
    f_hbm, x_hbm, b_hbm, stiff_hbm, cross_hbm, anchors_hbm,
    out_x, out_r,
    stiff, cross, anchors,
    XS, FS, BS, X, Z, U, Y, W, V, R, DG, INV, WR, WD, WG, C, K, TE, KS,
    PS, HT, HB, BO, BT, PW, PI, *rest,
):
    n_stages = len(stages)
    totals_out, totals_in = rest[:n_stages], rest[n_stages : 2 * n_stages]
    load_sem, send_sem, recv_sem, tsend_sem, trecv_sem = rest[2 * n_stages :]
    sections = TE.shape[0]
    groups = sections // 8
    g, r = lax.axis_index("gz"), lax.axis_index("rows")
    has_prev, has_next, has_above, has_below = g > 0, g < n_gz - 1, r > 0, r < n_rows - 1
    prev, nxt = {"gz": g - 1, "rows": r}, {"gz": g + 1, "rows": r}
    above, below = {"gz": g, "rows": r - 1}, {"gz": g, "rows": r + 1}

    loads = [
        pltpu.make_async_copy(src, dst, load_sem.at[i])
        for i, (src, dst) in enumerate(
            [(stiff_hbm, stiff), (cross_hbm, cross), (anchors_hbm, anchors), (b_hbm, BS), (x_hbm, XS), (f_hbm, FS)]
        )
    ]
    for load in loads:
        load.start()

    ny, nz, nc = digit_sizes(n_gz)
    my_digits = (g // (nz * nc), (g // nc) % nz, g % nc, r)

    def member(offset):
        y, z, c, x = [(d + o) % n for d, o, n in zip(my_digits, offset, (ny, nz, nc, n_rows))]
        return {"gz": (y * nz + z) * nc + c, "rows": x}

    barrier = pltpu.get_barrier_semaphore()
    for here, device in ((has_prev, prev), (has_next, nxt), (has_above, above), (has_below, below)):

        @pl.when(here)
        def _():
            pl.semaphore_signal(barrier, inc=1, device_id=device, device_id_type=MESH)

    for group in stages:
        for offset in group:
            pl.semaphore_signal(barrier, inc=1, device_id=member(offset), device_id_type=MESH)

    lane = lax.broadcasted_iota(jnp.int32, (8, LANES), 1)
    sub = lax.broadcasted_iota(jnp.int32, (8, LANES), 0)
    lo = lane < GRID
    column = lane % GRID
    open_column = column < GRID - 1
    inner_row = (2 * sub + lane // GRID) < 15
    mask_right = jnp.where(open_column, 1, 0)
    mask_down = jnp.where(inner_row, 2, 0)
    mask_diag = jnp.where(open_column & inner_row, 4, 0)
    down_scale = jnp.where(lo, 0.25, 1.0).astype(jnp.float32)
    zero = jnp.zeros((8, LANES), jnp.float32)

    def half(v):
        return pltpu.roll(v, GRID, 1)

    def left(v):
        return pltpu.roll(v, LANES - 1, 1)

    def right(v):
        return pltpu.roll(v, 1, 1)

    def from_up(v):
        turned = half(v)
        return jnp.where(lo, pltpu.roll(turned, 1, 0), turned)

    def from_down(v):
        turned = half(v)
        return jnp.where(lo, turned, pltpu.roll(turned, 7, 0))

    def tile(s):
        return pl.ds(pl.multiple_of(8 * s, 8), 8)

    def raw(s):
        return pl.ds((s // 8) * 64 + s % 8, 8, stride=8)

    def pack_last(a, b):
        return jnp.where(lo, half(a), b)

    def pack_first(a, b):
        return jnp.where(lo, a, half(b))

    def last_rows(q):
        return pl.ds(64 * q + 7, 8, stride=8)

    def first_rows(q):
        return pl.ds(64 * q, 8, stride=8)

    loads[2].wait()
    base = g * sections

    def anchor_step(i, hits):
        a = anchors[i] - base
        return tuple(jnp.where(sub + 8 * q == a, 1, hit) for q, hit in enumerate(hits))

    hits = lax.fori_loop(0, n_anchors, anchor_step, tuple(jnp.zeros((8, LANES), jnp.int32) for _ in range(groups)))
    for q in range(groups):
        TE[8 * q : 8 * q + 8, :] = jnp.where(hits[q] > 0, damping + anchor_stiffness, damping).astype(jnp.float32)

    loads[0].wait()
    loads[1].wait()
    loads[3].wait()

    def weights(s):
        bits = BS[raw(s), :]
        k = jnp.full((8, LANES), stiff[s], jnp.float32)
        KS[pl.ds(s, 1), :] = jnp.full((1, LANES), stiff[s], jnp.float32)
        WR[tile(s), :] = jnp.where((bits & mask_right) != 0, k, zero)
        WD[tile(s), :] = jnp.where((bits & mask_down) != 0, k, zero)
        WG[tile(s), :] = jnp.where((bits & mask_diag) != 0, k, zero)
        for j in range(PRED):
            kj = jnp.where(base + s > j, cross[j, s], 0.0)
            K[j, tile(s), :] = jnp.where((bits & (8 << j)) != 0, jnp.full((8, LANES), kj, jnp.float32), zero)

    for s in range(PRED):
        weights(s)

    for q in range(groups // 2):
        a = BS[64 * q + 56 : 64 * q + 64, :]
        b = BS[64 * (q + groups // 2) + 56 : 64 * (q + groups // 2) + 64, :]
        BO[8 * q : 8 * q + 8, :] = jnp.where(lo, half(a), b)

    loads[4].wait()
    for c in range(2):
        for s in list(range(PRED)) + list(range(sections - PRED, sections)):
            X[c, 8 * (s + PRED) : 8 * (s + PRED) + 8, :] = XS[c, pl.ds((s // 8) * 64 + s % 8, 8, stride=8), :]
    for q in range(groups):
        rows = slice(8 * q, 8 * q + 8)
        PS[0, 0, rows, :] = pack_first(XS[0, 64 * q : 64 * q + 8, :], XS[1, 64 * q : 64 * q + 8, :])
        PS[0, 1, rows, :] = pack_last(XS[0, 64 * q + 56 : 64 * q + 64, :], XS[1, 64 * q + 56 : 64 * q + 64, :])

    near = sum(jnp.where(here, 1, 0) for here in (has_prev, has_next, has_above, has_below))
    pl.semaphore_wait(barrier, near + sum(len(group) for group in stages))

    def remote(src, dst, at, device):
        return pltpu.make_async_remote_copy(
            src_ref=src, dst_ref=dst, send_sem=send_sem.at[at], recv_sem=recv_sem.at[at],
            device_id=device, device_id_type=MESH,
        )

    edge = 8 * PRED
    own = 8 * sections

    def row_copies(t):
        return (
            (has_below, has_above, remote(PS.at[t, 1], HT.at[t], 4 * t, below)),
            (has_above, has_below, remote(PS.at[t, 0], HB.at[t], 4 * t + 1, above)),
        )

    def section_copies(t):
        v = (X, Z, U)[t]
        return (
            (has_next, has_prev, remote(v.at[:, pl.ds(own, edge)], v.at[:, pl.ds(0, edge)], 4 * t + 2, nxt)),
            (has_prev, has_next, remote(v.at[:, pl.ds(edge, edge)], v.at[:, pl.ds(own + edge, edge)], 4 * t + 3, prev)),
        )

    bits_copy = (has_below, has_above, remote(BO, BT, 12, below))
    cross_copy = (has_prev, has_next, remote(K.at[:, pl.ds(0, edge)], K.at[:, pl.ds(own, edge)], 13, prev))

    def start(copies):
        for sends, _, copy in copies:
            pl.when(sends)(copy.start)

    def arrive(copies):
        for _, receives, copy in copies:
            pl.when(receives)(copy.wait_recv)

    def sent(copies):
        for sends, _, copy in copies:
            pl.when(sends)(copy.wait_send)

    start(row_copies(0) + (bits_copy, cross_copy) + section_copies(0))

    wide = jnp.zeros((2, edge, LANES), jnp.float32)

    @pl.when(jnp.logical_not(has_prev))
    def _():
        for v in (X, Z, U):
            v[:, 0:edge, :] = wide

    @pl.when(jnp.logical_not(has_next))
    def _():
        for v in (X, Z, U):
            v[:, own + edge : own + 2 * edge, :] = wide
        K[:, own : own + edge, :] = jnp.zeros((PRED, edge, LANES), jnp.float32)

    @pl.when(jnp.logical_not(has_above))
    def _():
        HT[...] = jnp.zeros(HT.shape, jnp.float32)
        BT[...] = jnp.zeros(BT.shape, jnp.int32)

    @pl.when(jnp.logical_not(has_below))
    def _():
        HB[...] = jnp.zeros(HB.shape, jnp.float32)

    ends = list(range(PRED)) + list(range(sections - PRED, sections))
    inner = sections - 2 * PRED
    unroll = next(n for n in (3, 2, 1) if inner % n == 0)

    def over_inner(body, carry):
        def step(i, carry):
            for n in range(unroll):
                carry = body(PRED + unroll * i + n, carry)
            return carry

        return lax.fori_loop(0, inner // unroll, step, carry)

    def fill(s, carry):
        weights(s)
        for c in range(2):
            X[c, tile(s + PRED), :] = XS[c, raw(s), :]
        return carry

    over_inner(fill, 0)
    for s in range(sections - PRED, sections):
        weights(s)

    def plane(v0, v1, wr, wd, wg):
        right0, right1 = wr * (v0 - left(v0)), (0.25 * wr) * (v1 - left(v1))
        under0, under1 = from_down(v0), from_down(v1)
        down0, down1 = (0.25 * wd) * (v0 - under0), wd * (v1 - under1)
        gap0, gap1 = v0 - left(under0), v1 - left(under1)
        near_, far_ = 0.625 * wg, 0.375 * wg
        diag0, diag1 = near_ * gap0 + far_ * gap1, far_ * gap0 + near_ * gap1
        pull0 = (right0 + down0 + diag0) - right(right0) - from_up(down0 + right(diag0))
        pull1 = (right1 + down1 + diag1) - right(right1) - from_up(down1 + right(diag1))
        return pull0, pull1

    def apply(v, out, s, first=False):
        wr, wd, wg = WR[tile(s), :], WD[tile(s), :], WG[tile(s), :]
        back = [K[j, tile(s), :] for j in range(PRED)]
        ahead = [K[j, tile(s + j + 1), :] for j in range(PRED)]
        if first:
            tether = jnp.broadcast_to(TE[pl.ds(s, 1), :], (8, LANES))
            centre = tether + ((back[0] + ahead[0]) + (back[1] + ahead[1]) + (back[2] + ahead[2]))
            C[tile(s), :] = centre
            shared = centre + 0.625 * (wg + right(from_up(wg)))
            across, along = wr + right(wr), wd + from_up(wd)
            DG[0, tile(s), :] = shared + across + 0.25 * along
            DG[1, tile(s), :] = shared + 0.25 * across + along
        else:
            centre = C[tile(s), :]
        mine = [v[c, tile(s + PRED), :] for c in range(2)]
        done = []
        for c, pull in enumerate(plane(*mine, wr, wd, wg)):
            total = pull + centre * mine[c]
            for j in range(PRED):
                total = total - (
                    back[j] * v[c, tile(s + PRED - j - 1), :] + ahead[j] * v[c, tile(s + PRED + j + 1), :]
                )
            out[c, tile(s), :] = total
            done.append(total)
        return mine[0] * done[0] + mine[1] * done[1]

    def first_apply(s, carry):
        apply(X, Y, s, first=True)
        return carry

    over_inner(first_apply, 0)

    def bottom_weights(q, carry):
        rows = tile(q)
        bits = BS[pl.ds(pl.multiple_of(64 * q + 56, 8), 8), :]
        bits = jnp.where(lo, half(bits), bits)
        k = jnp.where(has_below, KS[rows, :], zero)
        PW[2, rows, :] = jnp.where((bits & 2) != 0, k, zero) * down_scale
        PW[3, rows, :] = jnp.where(((bits & 4) != 0) & open_column, k, zero)
        return carry

    lax.fori_loop(0, groups, bottom_weights, 0)

    arrive((bits_copy,))

    def top_weights(q, carry):
        both = BT[tile(q), :]
        for n, bits in enumerate((jnp.where(lo, both, half(both)), jnp.where(lo, half(both), both))):
            rows = tile(q + n * (groups // 2))
            k = jnp.where(has_above, KS[rows, :], zero)
            PW[0, rows, :] = jnp.where((bits & 2) != 0, k, zero) * down_scale
            PW[1, rows, :] = jnp.where(((bits & 4) != 0) & open_column, k, zero)
        return carry

    lax.fori_loop(0, groups // 2, top_weights, 0)

    def outside(t, q):
        rows = tile(q)
        mine, other = PS[t, 0, rows, :], HT[t, rows, :]
        gap = other - left(mine)
        top = PW[0, rows, :] * (mine - other) - right(PW[1, rows, :] * (0.625 * gap + 0.375 * half(gap)))
        mine, other = PS[t, 1, rows, :], HB[t, rows, :]
        gap = mine - left(other)
        bottom = PW[2, rows, :] * (mine - other) + PW[3, rows, :] * (0.625 * gap + 0.375 * half(gap))
        return top, bottom

    def add_rows(ref, q, top, bottom):
        a, b = ref[0, first_rows(q), :], ref[1, first_rows(q), :]
        a, b = a + jnp.where(lo, top, zero), b + jnp.where(lo, half(top), zero)
        ref[0, first_rows(q), :] = a
        ref[1, first_rows(q), :] = b
        first = pack_first(a, b)
        a, b = ref[0, last_rows(q), :], ref[1, last_rows(q), :]
        a, b = a + jnp.where(lo, zero, half(bottom)), b + jnp.where(lo, zero, bottom)
        ref[0, last_rows(q), :] = a
        ref[1, last_rows(q), :] = b
        return first, pack_last(a, b)

    arrive((cross_copy,) + section_copies(0))
    for s in ends:
        first_apply(s, 0)
    arrive(row_copies(0))

    def edge_residual(q, carry):
        rows = tile(q)
        top, bottom = outside(0, q)
        y = add_rows(Y, q, top, bottom)
        d = add_rows(
            DG, q, PW[0, rows, :] + 0.625 * right(PW[1, rows, :]), PW[2, rows, :] + 0.625 * PW[3, rows, :]
        )
        head = pl.ds(pl.multiple_of(64 * q, 8), 8)
        foot = pl.ds(pl.multiple_of(64 * q + 56, 8), 8)
        f = (pack_first(FS[0, head, :], FS[1, head, :]), pack_last(FS[0, foot, :], FS[1, foot, :]))
        for n in range(2):
            inverse = 1.0 / d[n]
            PI[n, rows, :] = inverse
            PS[1, n, rows, :] = (f[n] - y[n]) * inverse
        return carry

    loads[5].wait()
    lax.fori_loop(0, groups, edge_residual, 0)
    start(row_copies(1))

    def residual(s, total):
        for c in range(2):
            inverse = 1.0 / DG[c, tile(s), :]
            res = FS[c, raw(s), :] - Y[c, tile(s), :]
            pre = res * inverse
            INV[c, tile(s), :] = inverse
            R[c, tile(s), :] = res
            Z[c, tile(s + PRED), :] = pre
            total = total + res * pre
        return total

    sum0 = zero
    for s in ends:
        sum0 = residual(s, sum0)
    start(section_copies(1))
    sum0 = over_inner(residual, sum0)

    def second_apply(s, carry):
        apply(Z, W, s)
        return carry

    over_inner(second_apply, 0)

    arrive(section_copies(1))
    for s in ends:
        second_apply(s, 0)
    arrive(row_copies(1))

    def edge_second(q, carry):
        rows = tile(q)
        w = add_rows(W, q, *outside(1, q))
        for n in range(2):
            PS[2, n, rows, :] = w[n] * PI[n, rows, :]
        return carry

    lax.fori_loop(0, groups, edge_second, 0)
    start(row_copies(2))

    def second(s, totals):
        sum1, sum2 = totals
        for c in range(2):
            w = W[c, tile(s), :]
            u = w * INV[c, tile(s), :]
            U[c, tile(s + PRED), :] = u
            sum1 = sum1 + w * Z[c, tile(s + PRED), :]
            sum2 = sum2 + w * u
        return sum1, sum2

    sums = (zero, zero)
    for s in ends:
        sums = second(s, sums)
    start(section_copies(2))
    sum1, sum2 = over_inner(second, sums)
    sum3 = over_inner(lambda s, total: total + apply(U, V, s), zero)

    arrive(section_copies(2))
    for s in ends:
        sum3 = sum3 + apply(U, V, s)
    arrive(row_copies(2))

    def edge_third(q, total):
        rows = tile(q)
        top, bottom = outside(2, q)
        add_rows(V, q, top, bottom)
        return total + (top * PS[2, 0, rows, :] + bottom * PS[2, 1, rows, :])

    sum3 = lax.fori_loop(0, groups, edge_third, sum3)

    row = zero
    for n, part in enumerate((sum0, sum1, sum2, sum3)):
        part = part + half(part)
        part = part + pltpu.roll(part, 32, 1)
        row = jnp.where(lane // 32 == n, part, row)
    row = jnp.sum(row, axis=0, keepdims=True)
    pending = []
    for t, group in enumerate(stages):
        totals_out[t][0] = row
        for n, offset in enumerate(group):
            copy = pltpu.make_async_remote_copy(
                src_ref=totals_out[t].at[0], dst_ref=totals_in[t].at[n],
                send_sem=tsend_sem.at[t], recv_sem=trecv_sem.at[t],
                device_id=member(offset), device_id_type=MESH,
            )
            copy.start()
        everyone = pltpu.make_async_remote_copy(
            src_ref=totals_in[t], dst_ref=totals_in[t], send_sem=tsend_sem.at[t], recv_sem=trecv_sem.at[t],
            device_id=member(group[0]), device_id_type=MESH,
        )
        everyone.wait_recv()
        pending.append(everyone)
        row = row + jnp.sum(totals_in[t][...], axis=0)

    lanes = lax.broadcasted_iota(jnp.int32, (1, LANES), 1) // 32
    c0, c1, c2, c3 = [jnp.sum(jnp.where(lanes == n, row, 0.0), axis=1, keepdims=True) for n in range(4)]
    alpha0 = c0 / c1
    inner1 = alpha0 * alpha0 * c2 - c0
    growth = 1.0 + inner1 / c0
    alpha1 = inner1 / (growth * growth * c1 - 2.0 * growth * alpha0 * c2 + alpha0 * alpha0 * c3)
    along = jnp.broadcast_to(alpha0 + alpha1 * growth, (8, LANES))
    against = jnp.broadcast_to(alpha1 * alpha0, (8, LANES))

    def finish(q, carry):
        for n in range(8):
            s = 8 * q + n
            for c in range(2):
                to = pl.ds(64 * q + n, 8, stride=8)
                z, u = Z[c, tile(s + PRED), :], U[c, tile(s + PRED), :]
                out_x[c, to, :] = X[c, tile(s + PRED), :] + (along * z - against * u)
                out_r[c, to, :] = R[c, tile(s), :] - (along * W[c, tile(s), :] - against * V[c, tile(s), :])
        return carry

    lax.fori_loop(0, groups, finish, 0)

    for t in range(3):
        sent(row_copies(t) + section_copies(t))
    sent((bits_copy, cross_copy))
    for copy in pending:
        copy.wait_send()


def tiles(shard):
    *lead, sections, nodes = shard.shape
    split = shard.reshape(*lead, sections // 8, 8, nodes // LANES, LANES)
    return jnp.swapaxes(split, -3, -2).reshape(*lead, sections * nodes // LANES, LANES)


def untiled(rows, sections, nodes):
    lead = rows.shape[:-2]
    split = rows.reshape(*lead, sections // 8, nodes // LANES, 8, LANES)
    return jnp.swapaxes(split, -3, -2).reshape(*lead, sections, nodes)


def per_device(n_gz, n_rows, forces, start, spring_bits, plane_stiffness, cross_weight, anchors):
    _, sections, nodes = forces.shape
    stages = stage_groups(n_gz, n_rows)
    f32 = functools.partial(pltpu.VMEM, dtype=jnp.float32)
    own, held = 8 * sections, 8 * (sections + 2 * PRED)
    scratch = [
        pltpu.SMEM((sections,), jnp.float32),
        pltpu.SMEM((PRED, sections), jnp.float32),
        pltpu.SMEM(anchors.shape, jnp.int32),
        f32((2, own, LANES)),
        f32((2, own, LANES)),
        pltpu.VMEM((own, LANES), jnp.int32),
        *[f32((2, held, LANES)) for _ in range(3)],
        *[f32((2, own, LANES)) for _ in range(6)],
        *[f32((own, LANES)) for _ in range(4)],
        f32((PRED, own + 8 * PRED, LANES)),
        f32((sections, LANES)),
        f32((sections, LANES)),
        f32((3, 2, sections, LANES)),
        f32((3, sections, LANES)),
        f32((3, sections, LANES)),
        pltpu.VMEM((sections // 2, LANES), jnp.int32),
        pltpu.VMEM((sections // 2, LANES), jnp.int32),
        f32((4, sections, LANES)),
        f32((2, sections, LANES)),
        *[f32((1, 1, LANES)) for _ in stages],
        *[f32((len(group), 1, LANES)) for group in stages],
        pltpu.SemaphoreType.DMA((6,)),
        pltpu.SemaphoreType.DMA((14,)),
        pltpu.SemaphoreType.DMA((14,)),
        pltpu.SemaphoreType.DMA((len(stages),)),
        pltpu.SemaphoreType.DMA((len(stages),)),
    ]
    shape = jax.ShapeDtypeStruct((2, own, LANES), jnp.float32)
    solved, left_over = pl.pallas_call(
        functools.partial(kernel, n_gz, n_rows, anchors.shape[0], stages),
        out_shape=(shape, shape),
        in_specs=[pl.BlockSpec(memory_space=pl.ANY)] * 6,
        out_specs=[pl.BlockSpec(memory_space=pltpu.VMEM)] * 2,
        scratch_shapes=scratch,
        compiler_params=pltpu.CompilerParams(
            collective_id=0, has_side_effects=True, vmem_limit_bytes=40 * 1024 * 1024
        ),
        name="cg",
    )(tiles(forces), tiles(start), tiles(spring_bits), plane_stiffness, cross_weight, anchors)
    return untiled(solved, sections, nodes), untiled(left_over, sections, nodes)


def solution(mesh):
    return jax.shard_map(
        functools.partial(per_device, mesh.shape["gz"], mesh.shape["rows"]),
        mesh=mesh,
        in_specs=(P(None, "gz", "rows"), P(None, "gz", "rows"), P("gz", "rows"), P("gz"), P(None, "gz"), P()),
        out_specs=(P(None, "gz", "rows"), P(None, "gz", "rows")),
        check_vma=False,
    )
```

time: 139 us -> 70 us (0.50)
  Pallas kernels: 0 us -> 63.5 us
  blocking collectives: 51.8 us -> 0 us
  starting transfers between devices: 39.7 us -> 0 us
  other arithmetic: 22.1 us -> 0 us
  between operations: 7.06 us -> 0.67 us
  waiting for transfers between devices: 6.36 us -> 0 us
  local copies, waits for them, and re-layouts: 10.8 us -> 5.69 us
    pallas_call x0 -> x1, Pallas kernels: none -> 63.5 us  [per_device(): pl.pallas_call(functools.partial(kernel, n_gz, n_rows, anchors.shape[0],...]
    all_to_all x4 -> x0, blocking collectives: 51.8 us -> none  [from_everyone(): return lax.all_to_all(copies, axis, split_axis=0, concat_axis=0, tiled=True)]
    ppermute x14 -> x0, starting transfers between devices: 39.7 us -> none  [the longest x6 22.1 us: extended(): before = lax.ppermute(last, axis, up)]
    ppermute x14 -> x0, waiting for transfers between devices: 6.36 us -> none  [the longest x6 5.63 us: extended(): after = lax.ppermute(first, axis, down)]
    slice x13 -> x0, local copies, waits for them, and re-layouts: 5.65 us -> none  [the longest x4 2.17 us: extended(): last = lax.slice_in_dim(shard, length - width, length, axis=dim)]
    reduce_sum x6 -> x0, other arithmetic: 5.32 us -> none  [the longest x2 5.17 us: paired(): jnp.sum(residual * precond)]
    mul x11 -> x0, other arithmetic: 5.2 us -> none  [the longest x2 2.66 us: per_device(): precond = residual * inverse]
    another operation x10 -> x0, other arithmetic: 4.12 us -> none  [the longest x2 1.93 us: per_device(): jnp.stack([cross_weight[lag_index][:, None] * bit_plane(spring_bits, 3 +...]
  transfers between devices with their start and end apart: 14 -> 0, of which waited for: 3 -> 0; matrix products, arithmetic and copies ran while one was open for 7% -> 0% of each run, Pallas kernels for 0% -> 0%
where the time goes in v1:
time: 70 us; the launch traced here: 69.8 us
  Pallas kernels  63.5 us (91%)
  local copies, waits for them, and re-layouts  5.69 us (8%)
    pallas_call x1, Pallas kernels, per_device(): pl.pallas_call(functools.partial(kernel, n_gz, n_rows, anchors.shape[0],...  63.5 us
    unnamed x14, local copies, waits for them, and re-layouts  5.69 us

profile of v1, /device:TPU:1, one launch (start us, length us, event | category | flops | bytes accessed | tf_op | source)
XLA Modules:
  0.0 69.8 jit_solution(9991672867795943453)
XLA Ops:
  0.6 0.0 copy-start.3
  0.6 0.0 copy-start.4
  0.7 0.0 copy-start.5
  0.7 0.7 copy-done.3
  1.3 0.0 copy-done.4
  1.3 0.0 copy-done.5
  1.3 0.0 copy-start
  1.3 1.1 %copy-done = f32[2,96,1024]{2,1,0:T(8,128)S(1)} copy-done((f32[2,96,1024]{2,1,0:T(8,128)S(1)}, f32[2,96,1024]{2,1,0:T(8,128)}, u32[]{:S(2)}) %copy-start) | copy-done | bytes 786456
  2.5 0.0 copy-start.1
  2.5 1.1 %copy-done.1 = f32[2,96,1024]{2,1,0:T(8,128)S(1)} copy-done((f32[2,96,1024]{2,1,0:T(8,128)S(1)}, f32[2,96,1024]{2,1,0:T(8,128)}, u32[]{:S(2)}) %copy-start.1) | copy-done | bytes 786456
  3.6 0.0 copy-start.2
  3.6 1.0 %copy-done.2 = s32[96,1024]{1,0:T(8,128)S(1)} copy-done((s32[96,1024]{1,0:T(8,128)S(1)}, s32[96,1024]{1,0:T(8,128)}, u32[]{:S(2)}) %copy-start.2) | copy-done | bytes 393240
  4.6 63.5 %cg.1 = (f32[2,768,128]{2,1,0:T(8,128)S(1)}, f32[2,768,128]{2,1,0:T(8,128)S(1)}) custom-call(f32[2,768,128]{2,1,0:T(8,128)S(1)} %bitcast.25, f32[2,768,128]{2,1,0:T(8,128)S(1)} %bitcast.26, s32[768,128]{1,0:T(8,128)S(1)} %bitcast.29, f32[96]{0:T(128)S(1)} %copy-done.4, f32[3,96]{1,0:T(4,128)S(1)} %copy-done.3, s32[64]{0:T(128)S(1)} %copy-done.5), custom_call_target="tpu_custom_call" | custom-call | tf_op jit(solution)/shard_map/cg/pallas_call | solution.py:531
  68.0 0.9 %copy.10 = f32[2,96,1024]{2,1,0:T(8,128)} copy(f32[2,96,1024]{2,1,0:T(8,128)S(1)} %bitcast.28) | data formatting | bytes 1572864
  68.9 0.9 %copy.11 = f32[2,96,1024]{2,1,0:T(8,128)} copy(f32[2,96,1024]{2,1,0:T(8,128)S(1)} %bitcast.27) | data formatting | bytes 1572864
Async XLA Ops:
  0.6 0.7 copy-start.3
  0.6 0.7 copy-start.4
  0.7 0.7 copy-start.5
  1.3 1.1 %copy-start = (f32[2,96,1024]{2,1,0:T(8,128)S(1)}, f32[2,96,1024]{2,1,0:T(8,128)}, u32[]{:S(2)}) copy-start(f32[2,96,1024]{2,1,0:T(8,128)} %param.6) | copy-start | bytes 2359300
  2.5 1.1 %copy-start.1 = (f32[2,96,1024]{2,1,0:T(8,128)S(1)}, f32[2,96,1024]{2,1,0:T(8,128)}, u32[]{:S(2)}) copy-start(f32[2,96,1024]{2,1,0:T(8,128)} %param.7) | copy-start | bytes 2359300
  3.6 1.0 %copy-start.2 = (s32[96,1024]{1,0:T(8,128)S(1)}, s32[96,1024]{1,0:T(8,128)}, u32[]{:S(2)}) copy-start(s32[96,1024]{1,0:T(8,128)} %param.8) | copy-start | bytes 1179652

commit v2 on v1

--- a/solution.py
+++ b/solution.py
@@ -10,6 +10,7 @@
 GRID = 64
 PRED = 3
 LANES = 128
+APPLY_UNROLL = 10
 MESH = pl.DeviceIdType.MESH
 
 damping = 0.05
@@ -32,8 +33,8 @@
     f_hbm, x_hbm, b_hbm, stiff_hbm, cross_hbm, anchors_hbm,
     out_x, out_r,
     stiff, cross, anchors,
-    XS, FS, BS, X, Z, U, Y, W, V, R, DG, INV, WR, WD, WG, C, K, TE, KS,
-    PS, HT, HB, BO, BT, PW, PI, *rest,
+    XS, FS, BS, X, Z, U, Y, W, V, R, INV, DG, WP, K, TE, KS,
+    PS, HT, HB, BO, BT, PW, PI, PY, PH, PF, FX, *rest,
 ):
     n_stages = len(stages)
     totals_out, totals_in = rest[:n_stages], rest[n_stages : 2 * n_stages]
@@ -93,13 +94,8 @@
     def right(v):
         return pltpu.roll(v, 1, 1)
 
-    def from_up(v):
-        turned = half(v)
-        return jnp.where(lo, pltpu.roll(turned, 1, 0), turned)
-
-    def from_down(v):
-        turned = half(v)
-        return jnp.where(lo, turned, pltpu.roll(turned, 7, 0))
+    def lowered(v, by):
+        return pltpu.roll(jnp.where(lo, v, pltpu.roll(v, 1, 0)), by, 1)
 
     def tile(s):
         return pl.ds(pl.multiple_of(8 * s, 8), 8)
@@ -112,12 +108,6 @@
 
     def pack_first(a, b):
         return jnp.where(lo, a, half(b))
-
-    def last_rows(q):
-        return pl.ds(64 * q + 7, 8, stride=8)
-
-    def first_rows(q):
-        return pl.ds(64 * q, 8, stride=8)
 
     loads[2].wait()
     base = g * sections
@@ -134,19 +124,24 @@
     loads[1].wait()
     loads[3].wait()
 
-    def weights(s):
+    def cross_weights(s):
         bits = BS[raw(s), :]
-        k = jnp.full((8, LANES), stiff[s], jnp.float32)
         KS[pl.ds(s, 1), :] = jnp.full((1, LANES), stiff[s], jnp.float32)
-        WR[tile(s), :] = jnp.where((bits & mask_right) != 0, k, zero)
-        WD[tile(s), :] = jnp.where((bits & mask_down) != 0, k, zero)
-        WG[tile(s), :] = jnp.where((bits & mask_diag) != 0, k, zero)
         for j in range(PRED):
             kj = jnp.where(base + s > j, cross[j, s], 0.0)
             K[j, tile(s), :] = jnp.where((bits & (8 << j)) != 0, jnp.full((8, LANES), kj, jnp.float32), zero)
+        return bits
+
+    def plane_weights(s, bits):
+        k = jnp.full((8, LANES), stiff[s], jnp.float32)
+        wr = jnp.where((bits & mask_right) != 0, k, zero)
+        wd = jnp.where((bits & mask_down) != 0, k, zero)
+        wg = jnp.where((bits & mask_diag) != 0, k, zero)
+        for n, w in enumerate((wr, right(wr), wd, lowered(wd, GRID), wg, lowered(wg, GRID + 1))):
+            WP[n, tile(s), :] = w
 
     for s in range(PRED):
-        weights(s)
+        cross_weights(s)
 
     for q in range(groups // 2):
         a = BS[64 * q + 56 : 64 * q + 64, :]
@@ -228,9 +223,10 @@
 
     ends = list(range(PRED)) + list(range(sections - PRED, sections))
     inner = sections - 2 * PRED
-    unroll = next(n for n in (3, 2, 1) if inner % n == 0)
-
-    def over_inner(body, carry):
+
+    def over_inner(body, carry, most):
+        unroll = next(n for n in range(most, 0, -1) if inner % n == 0)
+
         def step(i, carry):
             for n in range(unroll):
                 carry = body(PRED + unroll * i + n, carry)
@@ -239,48 +235,53 @@
         return lax.fori_loop(0, inner // unroll, step, carry)
 
     def fill(s, carry):
-        weights(s)
+        plane_weights(s, cross_weights(s))
         for c in range(2):
             X[c, tile(s + PRED), :] = XS[c, raw(s), :]
         return carry
 
-    over_inner(fill, 0)
+    over_inner(fill, 0, 10)
+    for s in range(PRED):
+        plane_weights(s, BS[raw(s), :])
     for s in range(sections - PRED, sections):
-        weights(s)
-
-    def plane(v0, v1, wr, wd, wg):
-        right0, right1 = wr * (v0 - left(v0)), (0.25 * wr) * (v1 - left(v1))
-        under0, under1 = from_down(v0), from_down(v1)
-        down0, down1 = (0.25 * wd) * (v0 - under0), wd * (v1 - under1)
-        gap0, gap1 = v0 - left(under0), v1 - left(under1)
-        near_, far_ = 0.625 * wg, 0.375 * wg
-        diag0, diag1 = near_ * gap0 + far_ * gap1, far_ * gap0 + near_ * gap1
-        pull0 = (right0 + down0 + diag0) - right(right0) - from_up(down0 + right(diag0))
-        pull1 = (right1 + down1 + diag1) - right(right1) - from_up(down1 + right(diag1))
-        return pull0, pull1
+        plane_weights(s, cross_weights(s))
 
     def apply(v, out, s, first=False):
-        wr, wd, wg = WR[tile(s), :], WD[tile(s), :], WG[tile(s), :]
+        wr, wl, wd, wu, wg, wv = [WP[n, tile(s), :] for n in range(6)]
         back = [K[j, tile(s), :] for j in range(PRED)]
         ahead = [K[j, tile(s + j + 1), :] for j in range(PRED)]
         if first:
             tether = jnp.broadcast_to(TE[pl.ds(s, 1), :], (8, LANES))
-            centre = tether + ((back[0] + ahead[0]) + (back[1] + ahead[1]) + (back[2] + ahead[2]))
-            C[tile(s), :] = centre
-            shared = centre + 0.625 * (wg + right(from_up(wg)))
-            across, along = wr + right(wr), wd + from_up(wd)
-            DG[0, tile(s), :] = shared + across + 0.25 * along
-            DG[1, tile(s), :] = shared + 0.25 * across + along
+            shared = tether + ((back[0] + ahead[0]) + (back[1] + ahead[1]) + (back[2] + ahead[2]))
+            shared = shared + 0.625 * (wg + wv)
+            across, along = wr + wl, wd + wu
+            own_weight = [shared + across + 0.25 * along, shared + 0.25 * across + along]
+            mixed = 0.375 * (wg + wv)
+            DG[2, tile(s), :] = mixed
+            for c in range(2):
+                DG[c, tile(s), :] = own_weight[c]
+                INV[c, tile(s), :] = 1.0 / own_weight[c]
         else:
-            centre = C[tile(s), :]
+            own_weight, mixed = [DG[c, tile(s), :] for c in range(2)], DG[2, tile(s), :]
         mine = [v[c, tile(s + PRED), :] for c in range(2)]
+        sides, lines, slants = [], [], []
+        for c in range(2):
+            after = jnp.where(lo, v[c, pl.ds(8 * (s + PRED) + 1, 8), :], mine[c])
+            before = jnp.where(lo, mine[c], v[c, pl.ds(8 * (s + PRED) - 1, 8), :])
+            sides.append(wr * left(mine[c]) + wl * right(mine[c]))
+            lines.append(wd * half(after) + wu * half(before))
+            slants.append(wg * pltpu.roll(after, GRID - 1, 1) + wv * pltpu.roll(before, GRID + 1, 1))
+        pulls = [
+            (sides[0] + 0.25 * lines[0]) + (0.625 * slants[0] + 0.375 * slants[1]),
+            (0.25 * sides[1] + lines[1]) + (0.375 * slants[0] + 0.625 * slants[1]),
+        ]
         done = []
-        for c, pull in enumerate(plane(*mine, wr, wd, wg)):
-            total = pull + centre * mine[c]
-            for j in range(PRED):
-                total = total - (
-                    back[j] * v[c, tile(s + PRED - j - 1), :] + ahead[j] * v[c, tile(s + PRED + j + 1), :]
-                )
+        for c in range(2):
+            ties = [
+                back[j] * v[c, tile(s + PRED - j - 1), :] + ahead[j] * v[c, tile(s + PRED + j + 1), :]
+                for j in range(PRED)
+            ]
+            total = (own_weight[c] * mine[c] + mixed * mine[1 - c]) - (pulls[c] + (ties[0] + ties[1] + ties[2]))
             out[c, tile(s), :] = total
             done.append(total)
         return mine[0] * done[0] + mine[1] * done[1]
@@ -289,85 +290,103 @@
         apply(X, Y, s, first=True)
         return carry
 
-    over_inner(first_apply, 0)
-
-    def bottom_weights(q, carry):
-        rows = tile(q)
-        bits = BS[pl.ds(pl.multiple_of(64 * q + 56, 8), 8), :]
+    over_inner(first_apply, 0, APPLY_UNROLL)
+
+    def rows_of(q):
+        return slice(8 * q, 8 * q + 8)
+
+    def packed(ref, q):
+        at = [[ref[c, pl.ds(64 * q + line, 8, stride=8), :] for c in range(2)] for line in (0, 7)]
+        return pack_first(*at[0]), pack_last(*at[1])
+
+    def spread(top, bottom):
+        return (top, half(top)), (half(bottom), bottom)
+
+    def change_rows(ref, q, top, bottom, change):
+        for line, keep_lo, parts in zip((0, 7), (False, True), spread(top, bottom)):
+            for c in range(2):
+                to = pl.ds(64 * q + line, 8, stride=8)
+                old = ref[c, to, :]
+                new = change(old, parts[c])
+                ref[c, to, :] = jnp.where(lo, old, new) if keep_lo else jnp.where(lo, new, old)
+
+    for q in range(groups):
+        rows = rows_of(q)
+        bits = BS[64 * q + 56 : 64 * q + 64, :]
         bits = jnp.where(lo, half(bits), bits)
         k = jnp.where(has_below, KS[rows, :], zero)
         PW[2, rows, :] = jnp.where((bits & 2) != 0, k, zero) * down_scale
         PW[3, rows, :] = jnp.where(((bits & 4) != 0) & open_column, k, zero)
-        return carry
-
-    lax.fori_loop(0, groups, bottom_weights, 0)
+
+    middle = range(1, groups - 1)
+    outer = sorted({0, groups - 1})
+
+    def before_rows(t, out, some):
+        for q in some:
+            rows = rows_of(q)
+            for n, part in enumerate(packed(out, q)):
+                PY[n, rows, :] = part
+                PH[n, rows, :] = half(PS[t, n, rows, :])
+
+    def outside(t, q):
+        rows = rows_of(q)
+        mine, turned, other = PS[t, 0, rows, :], PH[0, rows, :], HT[t, rows, :]
+        slant = 0.625 * (right(other) - mine) + 0.375 * (pltpu.roll(other, GRID + 1, 1) - turned)
+        top = PW[0, rows, :] * (mine - other) - PW[1, rows, :] * slant
+        mine, turned, other = PS[t, 1, rows, :], PH[1, rows, :], HB[t, rows, :]
+        slant = 0.625 * (mine - left(other)) + 0.375 * (turned - pltpu.roll(other, GRID - 1, 1))
+        bottom = PW[2, rows, :] * (mine - other) + PW[3, rows, :] * slant
+        FX[0, rows, :] = top
+        FX[1, rows, :] = bottom
+        return top, bottom
+
+    def add(old, new):
+        return old + new
+
+    def put(old, new):
+        return new
+
+    before_rows(0, Y, middle)
+    loads[5].wait()
+    for q in range(groups):
+        rows = rows_of(q)
+        head, foot = slice(64 * q, 64 * q + 8), slice(64 * q + 56, 64 * q + 64)
+        PF[0, rows, :] = pack_first(FS[0, head, :], FS[1, head, :])
+        PF[1, rows, :] = pack_last(FS[0, foot, :], FS[1, foot, :])
 
     arrive((bits_copy,))
-
-    def top_weights(q, carry):
-        both = BT[tile(q), :]
+    for q in range(groups // 2):
+        both = BT[rows_of(q), :]
         for n, bits in enumerate((jnp.where(lo, both, half(both)), jnp.where(lo, half(both), both))):
-            rows = tile(q + n * (groups // 2))
+            rows = rows_of(q + n * (groups // 2))
             k = jnp.where(has_above, KS[rows, :], zero)
             PW[0, rows, :] = jnp.where((bits & 2) != 0, k, zero) * down_scale
-            PW[1, rows, :] = jnp.where(((bits & 4) != 0) & open_column, k, zero)
-        return carry
-
-    lax.fori_loop(0, groups // 2, top_weights, 0)
-
-    def outside(t, q):
-        rows = tile(q)
-        mine, other = PS[t, 0, rows, :], HT[t, rows, :]
-        gap = other - left(mine)
-        top = PW[0, rows, :] * (mine - other) - right(PW[1, rows, :] * (0.625 * gap + 0.375 * half(gap)))
-        mine, other = PS[t, 1, rows, :], HB[t, rows, :]
-        gap = mine - left(other)
-        bottom = PW[2, rows, :] * (mine - other) + PW[3, rows, :] * (0.625 * gap + 0.375 * half(gap))
-        return top, bottom
-
-    def add_rows(ref, q, top, bottom):
-        a, b = ref[0, first_rows(q), :], ref[1, first_rows(q), :]
-        a, b = a + jnp.where(lo, top, zero), b + jnp.where(lo, half(top), zero)
-        ref[0, first_rows(q), :] = a
-        ref[1, first_rows(q), :] = b
-        first = pack_first(a, b)
-        a, b = ref[0, last_rows(q), :], ref[1, last_rows(q), :]
-        a, b = a + jnp.where(lo, zero, half(bottom)), b + jnp.where(lo, zero, bottom)
-        ref[0, last_rows(q), :] = a
-        ref[1, last_rows(q), :] = b
-        return first, pack_last(a, b)
+            PW[1, rows, :] = right(jnp.where(((bits & 4) != 0) & open_column, k, zero))
 
     arrive((cross_copy,) + section_copies(0))
     for s in ends:
         first_apply(s, 0)
+    before_rows(0, Y, outer)
+    for q in range(groups):
+        rows = rows_of(q)
+        top, bottom = packed(DG, q)
+        PI[0, rows, :] = 1.0 / (top + (PW[0, rows, :] + 0.625 * PW[1, rows, :]))
+        PI[1, rows, :] = 1.0 / (bottom + (PW[2, rows, :] + 0.625 * PW[3, rows, :]))
     arrive(row_copies(0))
-
-    def edge_residual(q, carry):
-        rows = tile(q)
-        top, bottom = outside(0, q)
-        y = add_rows(Y, q, top, bottom)
-        d = add_rows(
-            DG, q, PW[0, rows, :] + 0.625 * right(PW[1, rows, :]), PW[2, rows, :] + 0.625 * PW[3, rows, :]
-        )
-        head = pl.ds(pl.multiple_of(64 * q, 8), 8)
-        foot = pl.ds(pl.multiple_of(64 * q + 56, 8), 8)
-        f = (pack_first(FS[0, head, :], FS[1, head, :]), pack_last(FS[0, foot, :], FS[1, foot, :]))
-        for n in range(2):
-            inverse = 1.0 / d[n]
-            PI[n, rows, :] = inverse
-            PS[1, n, rows, :] = (f[n] - y[n]) * inverse
-        return carry
-
-    loads[5].wait()
-    lax.fori_loop(0, groups, edge_residual, 0)
+    for q in range(groups):
+        rows = rows_of(q)
+        for n, part in enumerate(outside(0, q)):
+            PS[1, n, rows, :] = (PF[n, rows, :] - (PY[n, rows, :] + part)) * PI[n, rows, :]
     start(row_copies(1))
+    for q in range(groups):
+        rows = rows_of(q)
+        change_rows(Y, q, FX[0, rows, :], FX[1, rows, :], add)
+        change_rows(INV, q, PI[0, rows, :], PI[1, rows, :], put)
 
     def residual(s, total):
         for c in range(2):
-            inverse = 1.0 / DG[c, tile(s), :]
             res = FS[c, raw(s), :] - Y[c, tile(s), :]
-            pre = res * inverse
-            INV[c, tile(s), :] = inverse
+            pre = res * INV[c, tile(s), :]
             R[c, tile(s), :] = res
             Z[c, tile(s + PRED), :] = pre
             total = total + res * pre
@@ -377,28 +396,27 @@
     for s in ends:
         sum0 = residual(s, sum0)
     start(section_copies(1))
-    sum0 = over_inner(residual, sum0)
+    sum0 = over_inner(residual, sum0, 10)
 
     def second_apply(s, carry):
         apply(Z, W, s)
         return carry
 
-    over_inner(second_apply, 0)
+    over_inner(second_apply, 0, APPLY_UNROLL)
+    before_rows(1, W, middle)
 
     arrive(section_copies(1))
     for s in ends:
         second_apply(s, 0)
+    before_rows(1, W, outer)
     arrive(row_copies(1))
-
-    def edge_second(q, carry):
-        rows = tile(q)
-        w = add_rows(W, q, *outside(1, q))
-        for n in range(2):
-            PS[2, n, rows, :] = w[n] * PI[n, rows, :]
-        return carry
-
-    lax.fori_loop(0, groups, edge_second, 0)
+    for q in range(groups):
+        rows = rows_of(q)
+        for n, part in enumerate(outside(1, q)):
+            PS[2, n, rows, :] = (PY[n, rows, :] + part) * PI[n, rows, :]
     start(row_copies(2))
+    for q in range(groups):
+        change_rows(W, q, FX[0, rows_of(q), :], FX[1, rows_of(q), :], add)
 
     def second(s, totals):
         sum1, sum2 = totals
@@ -414,21 +432,19 @@
     for s in ends:
         sums = second(s, sums)
     start(section_copies(2))
-    sum1, sum2 = over_inner(second, sums)
-    sum3 = over_inner(lambda s, total: total + apply(U, V, s), zero)
+    sum1, sum2 = over_inner(second, sums, 10)
+    sum3 = over_inner(lambda s, total: total + apply(U, V, s), zero, APPLY_UNROLL)
+    for q in range(groups):
+        for n in range(2):
+            PH[n, rows_of(q), :] = half(PS[2, n, rows_of(q), :])
 
     arrive(section_copies(2))
     for s in ends:
         sum3 = sum3 + apply(U, V, s)
     arrive(row_copies(2))
-
-    def edge_third(q, total):
-        rows = tile(q)
+    for q in range(groups):
         top, bottom = outside(2, q)
-        add_rows(V, q, top, bottom)
-        return total + (top * PS[2, 0, rows, :] + bottom * PS[2, 1, rows, :])
-
-    sum3 = lax.fori_loop(0, groups, edge_third, sum3)
+        sum3 = sum3 + (top * PS[2, 0, rows_of(q), :] + bottom * PS[2, 1, rows_of(q), :])
 
     row = zero
     for n, part in enumerate((sum0, sum1, sum2, sum3)):
@@ -437,6 +453,11 @@
         row = jnp.where(lane // 32 == n, part, row)
     row = jnp.sum(row, axis=0, keepdims=True)
     pending = []
+
+    def finish_rows():
+        for q in range(groups):
+            change_rows(V, q, FX[0, rows_of(q), :], FX[1, rows_of(q), :], add)
+
     for t, group in enumerate(stages):
         totals_out[t][0] = row
         for n, offset in enumerate(group):
@@ -450,6 +471,8 @@
             src_ref=totals_in[t], dst_ref=totals_in[t], send_sem=tsend_sem.at[t], recv_sem=trecv_sem.at[t],
             device_id=member(group[0]), device_id_type=MESH,
         )
+        if t == 0:
+            finish_rows()
         everyone.wait_recv()
         pending.append(everyone)
         row = row + jnp.sum(totals_in[t][...], axis=0)
@@ -507,8 +530,9 @@
         f32((2, own, LANES)),
         pltpu.VMEM((own, LANES), jnp.int32),
         *[f32((2, held, LANES)) for _ in range(3)],
-        *[f32((2, own, LANES)) for _ in range(6)],
-        *[f32((own, LANES)) for _ in range(4)],
+        *[f32((2, own, LANES)) for _ in range(5)],
+        f32((3, own, LANES)),
+        f32((6, own, LANES)),
         f32((PRED, own + 8 * PRED, LANES)),
         f32((sections, LANES)),
         f32((sections, LANES)),
@@ -518,7 +542,7 @@
         pltpu.VMEM((sections // 2, LANES), jnp.int32),
         pltpu.VMEM((sections // 2, LANES), jnp.int32),
         f32((4, sections, LANES)),
-        f32((2, sections, LANES)),
+        *[f32((2, sections, LANES)) for _ in range(5)],
         *[f32((1, 1, LANES)) for _ in stages],
         *[f32((len(group), 1, LANES)) for group in stages],
         pltpu.SemaphoreType.DMA((6,)),
@@ -530,12 +554,12 @@
     shape = jax.ShapeDtypeStruct((2, own, LANES), jnp.float32)
     solved, left_over = pl.pallas_call(
         functools.partial(kernel, n_gz, n_rows, anchors.shape[0], stages),
-        out_shape=(shape, shape),
-        in_specs=[pl.BlockSpec(memory_space=pl.ANY)] * 6,
+        out_shape=(pltpu.VMEM(shape.shape, jnp.float32),) * 2,
+        in_specs=[pl.BlockSpec(memory_space=pltpu.HBM)] * 6,
         out_specs=[pl.BlockSpec(memory_space=pltpu.VMEM)] * 2,
         scratch_shapes=scratch,
         compiler_params=pltpu.CompilerParams(
-            collective_id=0, has_side_effects=True, vmem_limit_bytes=40 * 1024 * 1024
+            collective_id=0, has_side_effects=True
         ),
         name="cg",
     )(tiles(forces), tiles(start), tiles(spring_bits), plane_stiffness, cross_weight, anchors)

time: 70 us -> 34.2 us (0.49)
  Pallas kernels: 63.5 us -> 31.7 us
  local copies, waits for them, and re-layouts: 5.69 us -> 1.76 us
    pallas_call x1, Pallas kernels: 63.5 us -> 31.7 us  [per_device(): pl.pallas_call(functools.partial(kernel, n_gz, n_rows, anchors.shape[0],...]
    unnamed x14 -> x2, local copies, waits for them, and re-layouts: 5.69 us -> 1.76 us
where the time goes in v2:
time: 34.2 us; the launch traced here: 34.1 us
  Pallas kernels  31.7 us (93%)
  local copies, waits for them, and re-layouts  1.76 us (5%)
  between operations  0.64 us (2%)
    pallas_call x1, Pallas kernels, per_device(): pl.pallas_call(functools.partial(kernel, n_gz, n_rows, anchors.shape[0],...  31.7 us
    unnamed x2, local copies, waits for them, and re-layouts  1.76 us

profile of v2, /device:TPU:1, one launch (start us, length us, event | category | flops | bytes accessed | tf_op | source)
XLA Modules:
  0.0 34.1 jit_solution(3755477413308462677)
XLA Ops:
  0.6 31.7 %cg.1 = (f32[2,768,128]{2,1,0:T(8,128)S(1)}, f32[2,768,128]{2,1,0:T(8,128)S(1)}) custom-call(f32[2,768,128]{2,1,0:T(8,128)} %bitcast.27, f32[2,768,128]{2,1,0:T(8,128)} %bitcast.28, s32[768,128]{1,0:T(8,128)} %bitcast.29, f32[96]{0:T(128)} %stiff_hbm.1, f32[3,96]{1,0:T(4,128)} %cross_hbm.1, s32[64]{0:T(128)} %anchors_hbm.1), custom_call_target="tpu_custom_call" | custom-call | tf_op jit(solution)/shard_map/cg/pallas_call | solution.py:555
  32.4 0.9 %copy.10 = f32[2,96,1024]{2,1,0:T(8,128)} copy(f32[2,96,1024]{2,1,0:T(8,128)S(1)} %bitcast.26) | data formatting | bytes 1572864
  33.3 0.9 %copy.11 = f32[2,96,1024]{2,1,0:T(8,128)} copy(f32[2,96,1024]{2,1,0:T(8,128)S(1)} %bitcast.25) | data formatting | bytes 1572864

commit v3 on v2

--- a/solution.py
+++ b/solution.py
@@ -10,7 +10,8 @@
 GRID = 64
 PRED = 3
 LANES = 128
-APPLY_UNROLL = 10
+APPLY_UNROLL = 18
+FILL_UNROLL = 18
 MESH = pl.DeviceIdType.MESH
 
 damping = 0.05
@@ -38,7 +39,7 @@
 ):
     n_stages = len(stages)
     totals_out, totals_in = rest[:n_stages], rest[n_stages : 2 * n_stages]
-    load_sem, send_sem, recv_sem, tsend_sem, trecv_sem = rest[2 * n_stages :]
+    load_sem, send_sem, recv_sem, tsend_sem, trecv_sem, word_sem = rest[2 * n_stages :]
     sections = TE.shape[0]
     groups = sections // 8
     g, r = lax.axis_index("gz"), lax.axis_index("rows")
@@ -49,18 +50,33 @@
     loads = [
         pltpu.make_async_copy(src, dst, load_sem.at[i])
         for i, (src, dst) in enumerate(
-            [(stiff_hbm, stiff), (cross_hbm, cross), (anchors_hbm, anchors), (b_hbm, BS), (x_hbm, XS), (f_hbm, FS)]
+            [(x_hbm, XS), (b_hbm, BS), (stiff_hbm, stiff), (cross_hbm, cross), (anchors_hbm, anchors), (f_hbm, FS)]
         )
     ]
     for load in loads:
         load.start()
 
     ny, nz, nc = digit_sizes(n_gz)
-    my_digits = (g // (nz * nc), (g // nc) % nz, g % nc, r)
+    my_digits = (g // (nz * nc), (g // nc) & (nz - 1), g & (nc - 1), r)
 
     def member(offset):
-        y, z, c, x = [(d + o) % n for d, o, n in zip(my_digits, offset, (ny, nz, nc, n_rows))]
+        y, z, c, x = [(d + o) & (n - 1) for d, o, n in zip(my_digits, offset, (ny, nz, nc, n_rows))]
         return {"gz": (y * nz + z) * nc + c, "rows": x}
+
+    def steps(size, by):
+        return sorted({step % size for step in by} - {0})
+
+    beside = [(y, 0, 0, 0) for y in steps(ny, (1, -1))] + [(0, z, 0, 0) for z in steps(nz, (1, -1))]
+    column_of = [(y, 0, 0, 0) for y in range(1, ny)]
+    word = (beside, column_of + [(0, z, 0, 0) for z in steps(nz, (2, -2))], column_of)
+
+    def say(t):
+        for offset in word[t]:
+            pl.semaphore_signal(word_sem.at[t], inc=1, device_id=member(offset), device_id_type=MESH)
+
+    def hear(t):
+        if word[t]:
+            pl.semaphore_wait(word_sem.at[t], len(word[t]))
 
     barrier = pltpu.get_barrier_semaphore()
     for here, device in ((has_prev, prev), (has_next, nxt), (has_above, above), (has_below, below)):
@@ -69,9 +85,9 @@
         def _():
             pl.semaphore_signal(barrier, inc=1, device_id=device, device_id_type=MESH)
 
-    for group in stages:
-        for offset in group:
-            pl.semaphore_signal(barrier, inc=1, device_id=member(offset), device_id_type=MESH)
+    greeted = stages[0] + beside
+    for offset in greeted:
+        pl.semaphore_signal(barrier, inc=1, device_id=member(offset), device_id_type=MESH)
 
     lane = lax.broadcasted_iota(jnp.int32, (8, LANES), 1)
     sub = lax.broadcasted_iota(jnp.int32, (8, LANES), 0)
@@ -109,20 +125,7 @@
     def pack_first(a, b):
         return jnp.where(lo, a, half(b))
 
-    loads[2].wait()
     base = g * sections
-
-    def anchor_step(i, hits):
-        a = anchors[i] - base
-        return tuple(jnp.where(sub + 8 * q == a, 1, hit) for q, hit in enumerate(hits))
-
-    hits = lax.fori_loop(0, n_anchors, anchor_step, tuple(jnp.zeros((8, LANES), jnp.int32) for _ in range(groups)))
-    for q in range(groups):
-        TE[8 * q : 8 * q + 8, :] = jnp.where(hits[q] > 0, damping + anchor_stiffness, damping).astype(jnp.float32)
-
-    loads[0].wait()
-    loads[1].wait()
-    loads[3].wait()
 
     def cross_weights(s):
         bits = BS[raw(s), :]
@@ -140,6 +143,8 @@
         for n, w in enumerate((wr, right(wr), wd, lowered(wd, GRID), wg, lowered(wg, GRID + 1))):
             WP[n, tile(s), :] = w
 
+    for load in loads[1:4]:
+        load.wait()
     for s in range(PRED):
         cross_weights(s)
 
@@ -148,7 +153,7 @@
         b = BS[64 * (q + groups // 2) + 56 : 64 * (q + groups // 2) + 64, :]
         BO[8 * q : 8 * q + 8, :] = jnp.where(lo, half(a), b)
 
-    loads[4].wait()
+    loads[0].wait()
     for c in range(2):
         for s in list(range(PRED)) + list(range(sections - PRED, sections)):
             X[c, 8 * (s + PRED) : 8 * (s + PRED) + 8, :] = XS[c, pl.ds((s // 8) * 64 + s % 8, 8, stride=8), :]
@@ -158,7 +163,7 @@
         PS[0, 1, rows, :] = pack_last(XS[0, 64 * q + 56 : 64 * q + 64, :], XS[1, 64 * q + 56 : 64 * q + 64, :])
 
     near = sum(jnp.where(here, 1, 0) for here in (has_prev, has_next, has_above, has_below))
-    pl.semaphore_wait(barrier, near + sum(len(group) for group in stages))
+    pl.semaphore_wait(barrier, near + len(greeted))
 
     def remote(src, dst, at, device):
         return pltpu.make_async_remote_copy(
@@ -197,7 +202,18 @@
         for sends, _, copy in copies:
             pl.when(sends)(copy.wait_send)
 
-    start(row_copies(0) + (bits_copy, cross_copy) + section_copies(0))
+    start(row_copies(0) + section_copies(0) + (cross_copy, bits_copy))
+    say(0)
+
+    loads[4].wait()
+
+    def anchor_step(i, hits):
+        a = anchors[i] - base
+        return tuple(jnp.where(sub + 8 * q == a, 1, hit) for q, hit in enumerate(hits))
+
+    hits = lax.fori_loop(0, n_anchors, anchor_step, tuple(jnp.zeros((8, LANES), jnp.int32) for _ in range(groups)))
+    for q in range(groups):
+        TE[8 * q : 8 * q + 8, :] = jnp.where(hits[q] > 0, damping + anchor_stiffness, damping).astype(jnp.float32)
 
     wide = jnp.zeros((2, edge, LANES), jnp.float32)
 
@@ -240,7 +256,7 @@
             X[c, tile(s + PRED), :] = XS[c, raw(s), :]
         return carry
 
-    over_inner(fill, 0, 10)
+    over_inner(fill, 0, FILL_UNROLL)
     for s in range(PRED):
         plane_weights(s, BS[raw(s), :])
     for s in range(sections - PRED, sections):
@@ -354,7 +370,8 @@
         PF[0, rows, :] = pack_first(FS[0, head, :], FS[1, head, :])
         PF[1, rows, :] = pack_last(FS[0, foot, :], FS[1, foot, :])
 
-    arrive((bits_copy,))
+    arrive((cross_copy,) + section_copies(0) + row_copies(0) + (bits_copy,))
+    hear(0)
     for q in range(groups // 2):
         both = BT[rows_of(q), :]
         for n, bits in enumerate((jnp.where(lo, both, half(both)), jnp.where(lo, half(both), both))):
@@ -363,7 +380,6 @@
             PW[0, rows, :] = jnp.where((bits & 2) != 0, k, zero) * down_scale
             PW[1, rows, :] = right(jnp.where(((bits & 4) != 0) & open_column, k, zero))
 
-    arrive((cross_copy,) + section_copies(0))
     for s in ends:
         first_apply(s, 0)
     before_rows(0, Y, outer)
@@ -372,12 +388,14 @@
         top, bottom = packed(DG, q)
         PI[0, rows, :] = 1.0 / (top + (PW[0, rows, :] + 0.625 * PW[1, rows, :]))
         PI[1, rows, :] = 1.0 / (bottom + (PW[2, rows, :] + 0.625 * PW[3, rows, :]))
-    arrive(row_copies(0))
     for q in range(groups):
         rows = rows_of(q)
         for n, part in enumerate(outside(0, q)):
-            PS[1, n, rows, :] = (PF[n, rows, :] - (PY[n, rows, :] + part)) * PI[n, rows, :]
+            res = PF[n, rows, :] - (PY[n, rows, :] + part)
+            PF[n, rows, :] = res
+            PS[1, n, rows, :] = res * PI[n, rows, :]
     start(row_copies(1))
+    say(1)
     for q in range(groups):
         rows = rows_of(q)
         change_rows(Y, q, FX[0, rows, :], FX[1, rows, :], add)
@@ -405,27 +423,28 @@
     over_inner(second_apply, 0, APPLY_UNROLL)
     before_rows(1, W, middle)
 
-    arrive(section_copies(1))
+    arrive(section_copies(1) + row_copies(1))
+    hear(1)
     for s in ends:
         second_apply(s, 0)
     before_rows(1, W, outer)
-    arrive(row_copies(1))
     for q in range(groups):
         rows = rows_of(q)
         for n, part in enumerate(outside(1, q)):
-            PS[2, n, rows, :] = (PY[n, rows, :] + part) * PI[n, rows, :]
+            PS[2, n, rows, :] = (PF[n, rows, :] - (PY[n, rows, :] + part)) * PI[n, rows, :]
     start(row_copies(2))
+    say(2)
     for q in range(groups):
         change_rows(W, q, FX[0, rows_of(q), :], FX[1, rows_of(q), :], add)
 
     def second(s, totals):
         sum1, sum2 = totals
         for c in range(2):
-            w = W[c, tile(s), :]
-            u = w * INV[c, tile(s), :]
+            gap = R[c, tile(s), :] - W[c, tile(s), :]
+            u = gap * INV[c, tile(s), :]
             U[c, tile(s + PRED), :] = u
-            sum1 = sum1 + w * Z[c, tile(s + PRED), :]
-            sum2 = sum2 + w * u
+            sum1 = sum1 + gap * Z[c, tile(s + PRED), :]
+            sum2 = sum2 + gap * u
         return sum1, sum2
 
     sums = (zero, zero)
@@ -438,10 +457,10 @@
         for n in range(2):
             PH[n, rows_of(q), :] = half(PS[2, n, rows_of(q), :])
 
-    arrive(section_copies(2))
+    arrive(section_copies(2) + row_copies(2))
+    hear(2)
     for s in ends:
         sum3 = sum3 + apply(U, V, s)
-    arrive(row_copies(2))
     for q in range(groups):
         top, bottom = outside(2, q)
         sum3 = sum3 + (top * PS[2, 0, rows_of(q), :] + bottom * PS[2, 1, rows_of(q), :])
@@ -478,13 +497,16 @@
         row = row + jnp.sum(totals_in[t][...], axis=0)
 
     lanes = lax.broadcasted_iota(jnp.int32, (1, LANES), 1) // 32
-    c0, c1, c2, c3 = [jnp.sum(jnp.where(lanes == n, row, 0.0), axis=1, keepdims=True) for n in range(4)]
-    alpha0 = c0 / c1
-    inner1 = alpha0 * alpha0 * c2 - c0
-    growth = 1.0 + inner1 / c0
-    alpha1 = inner1 / (growth * growth * c1 - 2.0 * growth * alpha0 * c2 + alpha0 * alpha0 * c3)
-    along = jnp.broadcast_to(alpha0 + alpha1 * growth, (8, LANES))
-    against = jnp.broadcast_to(alpha1 * alpha0, (8, LANES))
+    zz, zy, yy, ay = [jnp.sum(jnp.where(lanes == n, row, 0.0), axis=1, keepdims=True) for n in range(4)]
+    curve = zz - zy
+    alpha0 = zz / curve
+    turn = -zy / curve
+    inner1 = alpha0 * alpha0 * (yy - zy * zy / zz)
+    growth = inner1 / zz
+    bend = turn * turn * curve + 2.0 * turn * alpha0 * (zy - yy) + alpha0 * alpha0 * ay
+    alpha1 = inner1 / (bend - growth * inner1 / alpha0)
+    along = jnp.broadcast_to(alpha0 + alpha1 * (turn + growth), (8, LANES))
+    across = jnp.broadcast_to(alpha1 * alpha0, (8, LANES))
 
     def finish(q, carry):
         for n in range(8):
@@ -492,8 +514,8 @@
             for c in range(2):
                 to = pl.ds(64 * q + n, 8, stride=8)
                 z, u = Z[c, tile(s + PRED), :], U[c, tile(s + PRED), :]
-                out_x[c, to, :] = X[c, tile(s + PRED), :] + (along * z - against * u)
-                out_r[c, to, :] = R[c, tile(s), :] - (along * W[c, tile(s), :] - against * V[c, tile(s), :])
+                out_x[c, to, :] = X[c, tile(s + PRED), :] + (along * z + across * u)
+                out_r[c, to, :] = R[c, tile(s), :] - (along * W[c, tile(s), :] + across * V[c, tile(s), :])
         return carry
 
     lax.fori_loop(0, groups, finish, 0)
@@ -550,6 +572,7 @@
         pltpu.SemaphoreType.DMA((14,)),
         pltpu.SemaphoreType.DMA((len(stages),)),
         pltpu.SemaphoreType.DMA((len(stages),)),
+        pltpu.SemaphoreType.REGULAR((3,)),
     ]
     shape = jax.ShapeDtypeStruct((2, own, LANES), jnp.float32)
     solved, left_over = pl.pallas_call(

time: 34.2 us -> 32.7 us (0.956)
  Pallas kernels: 31.7 us -> 30.1 us
    pallas_call x1, Pallas kernels: 31.7 us -> 30.1 us  [per_device(): pl.pallas_call(functools.partial(kernel, n_gz, n_rows, anchors.shape[0],...]
where the time goes in v3:
time: 32.7 us; the launch traced here: 32.5 us
  Pallas kernels  30.1 us (92%)
  local copies, waits for them, and re-layouts  1.76 us (5%)
  between operations  0.64 us (2%)
    pallas_call x1, Pallas kernels, per_device(): pl.pallas_call(functools.partial(kernel, n_gz, n_rows, anchors.shape[0],...  30.1 us
    unnamed x2, local copies, waits for them, and re-layouts  1.76 us

profile of v3, /device:TPU:1, one launch (start us, length us, event | category | flops | bytes accessed | tf_op | source)
XLA Modules:
  0.0 32.5 jit_solution(17444527767720314525)
XLA Ops:
  0.6 30.1 %cg.1 = (f32[2,768,128]{2,1,0:T(8,128)S(1)}, f32[2,768,128]{2,1,0:T(8,128)S(1)}) custom-call(f32[2,768,128]{2,1,0:T(8,128)} %bitcast.27, f32[2,768,128]{2,1,0:T(8,128)} %bitcast.28, s32[768,128]{1,0:T(8,128)} %bitcast.29, f32[96]{0:T(128)} %stiff_hbm.1, f32[3,96]{1,0:T(4,128)} %cross_hbm.1, s32[64]{0:T(128)} %anchors_hbm.1), custom_call_target="tpu_custom_call" | custom-call | tf_op jit(solution)/shard_map/cg/pallas_call | solution.py:578
  30.8 0.9 %copy.10 = f32[2,96,1024]{2,1,0:T(8,128)} copy(f32[2,96,1024]{2,1,0:T(8,128)S(1)} %bitcast.26) | data formatting | bytes 1572864
  31.7 0.9 %copy.11 = f32[2,96,1024]{2,1,0:T(8,128)} copy(f32[2,96,1024]{2,1,0:T(8,128)S(1)} %bitcast.25) | data formatting | bytes 1572864

commit v4 on v3

--- a/solution.py
+++ b/solution.py
@@ -10,6 +10,7 @@
 GRID = 64
 PRED = 3
 LANES = 128
+PARTS = 3
 APPLY_UNROLL = 18
 FILL_UNROLL = 18
 MESH = pl.DeviceIdType.MESH
@@ -24,17 +25,21 @@
 
 def stage_groups(size, rows):
     ny, nz, nc = digit_sizes(size)
-    near = [(0, 0, c, x) for c in range(nc) for x in range(rows)][1:]
-    far = [(y, z, 0, 0) for y in range(ny) for z in range(nz)][1:]
-    return [group for group in (near, far) if group]
+    twin = [(0, 0, c, 0) for c in range(1, nc)]
+    rest = [(y, z, 0, x) for y in range(ny) for z in range(nz) for x in range(rows)][1:]
+
+    def hops(offset):
+        return sum(min(d, n - d) for d, n in zip(offset, (ny, nz, nc, rows)))
+
+    return [sorted(group, key=hops, reverse=True) for group in (twin, rest) if group]
 
 
 def kernel(
     n_gz, n_rows, n_anchors, stages,
     f_hbm, x_hbm, b_hbm, stiff_hbm, cross_hbm, anchors_hbm,
-    out_x, out_r,
+    X, Z, U, R, W, V, factors,
     stiff, cross, anchors,
-    XS, FS, BS, X, Z, U, Y, W, V, R, INV, DG, WP, K, TE, KS,
+    XS, FS, BS, Y, INV, DG, WP, K, TE, KS,
     PS, HT, HB, BO, BT, PW, PI, PY, PH, PF, FX, *rest,
 ):
     n_stages = len(stages)
@@ -50,10 +55,10 @@
     loads = [
         pltpu.make_async_copy(src, dst, load_sem.at[i])
         for i, (src, dst) in enumerate(
-            [(x_hbm, XS), (b_hbm, BS), (stiff_hbm, stiff), (cross_hbm, cross), (anchors_hbm, anchors), (f_hbm, FS)]
+            [(anchors_hbm, anchors), (stiff_hbm, stiff), (cross_hbm, cross), (b_hbm, BS), (x_hbm, XS), (f_hbm, FS)]
         )
     ]
-    for load in loads:
+    for load in loads[:5]:
         load.start()
 
     ny, nz, nc = digit_sizes(n_gz)
@@ -66,9 +71,9 @@
     def steps(size, by):
         return sorted({step % size for step in by} - {0})
 
-    beside = [(y, 0, 0, 0) for y in steps(ny, (1, -1))] + [(0, z, 0, 0) for z in steps(nz, (1, -1))]
-    column_of = [(y, 0, 0, 0) for y in range(1, ny)]
-    word = (beside, column_of + [(0, z, 0, 0) for z in steps(nz, (2, -2))], column_of)
+    beside = [(y, 0, 0, 0) for y in steps(ny, (1, -1))] + [(0, 0, 0, x) for x in steps(n_rows, (1, -1))]
+    beside += [(0, z, 0, 0) for z in steps(nz, (1, -1, 2, -2))]
+    word = (beside, [(0, 0, 0, x) for x in range(1, n_rows)], [(y, 0, 0, 0) for y in range(1, ny)])
 
     def say(t):
         for offset in word[t]:
@@ -127,6 +132,18 @@
 
     base = g * sections
 
+    loads[0].wait()
+
+    def anchor_step(i, hits):
+        for n in range(8):
+            a = anchors[8 * i + n] - base
+            hits = tuple(jnp.where(sub == a - 8 * q, 1, hit) for q, hit in enumerate(hits))
+        return hits
+
+    hits = lax.fori_loop(0, n_anchors // 8, anchor_step, tuple(jnp.zeros((8, LANES), jnp.int32) for _ in range(groups)))
+    for q in range(groups):
+        TE[8 * q : 8 * q + 8, :] = jnp.where(hits[q] > 0, damping + anchor_stiffness, damping).astype(jnp.float32)
+
     def cross_weights(s):
         bits = BS[raw(s), :]
         KS[pl.ds(s, 1), :] = jnp.full((1, LANES), stiff[s], jnp.float32)
@@ -153,7 +170,7 @@
         b = BS[64 * (q + groups // 2) + 56 : 64 * (q + groups // 2) + 64, :]
         BO[8 * q : 8 * q + 8, :] = jnp.where(lo, half(a), b)
 
-    loads[0].wait()
+    loads[4].wait()
     for c in range(2):
         for s in list(range(PRED)) + list(range(sections - PRED, sections)):
             X[c, 8 * (s + PRED) : 8 * (s + PRED) + 8, :] = XS[c, pl.ds((s // 8) * 64 + s % 8, 8, stride=8), :]
@@ -203,17 +220,8 @@
             pl.when(sends)(copy.wait_send)
 
     start(row_copies(0) + section_copies(0) + (cross_copy, bits_copy))
+    loads[5].start()
     say(0)
-
-    loads[4].wait()
-
-    def anchor_step(i, hits):
-        a = anchors[i] - base
-        return tuple(jnp.where(sub + 8 * q == a, 1, hit) for q, hit in enumerate(hits))
-
-    hits = lax.fori_loop(0, n_anchors, anchor_step, tuple(jnp.zeros((8, LANES), jnp.int32) for _ in range(groups)))
-    for q in range(groups):
-        TE[8 * q : 8 * q + 8, :] = jnp.where(hits[q] > 0, damping + anchor_stiffness, damping).astype(jnp.float32)
 
     wide = jnp.zeros((2, edge, LANES), jnp.float32)
 
@@ -494,7 +502,12 @@
             finish_rows()
         everyone.wait_recv()
         pending.append(everyone)
-        row = row + jnp.sum(totals_in[t][...], axis=0)
+        count = len(group)
+        cuts = [count * n // 6 for n in range(7)] if count > 30 else [0, count]
+        parts = [jnp.sum(totals_in[t][a:b], axis=0) for a, b in zip(cuts, cuts[1:])]
+        while len(parts) > 1:
+            parts = [sum(parts[n : n + 2][1:], parts[n]) for n in range(0, len(parts), 2)]
+        row = row + parts[0]
 
     lanes = lax.broadcasted_iota(jnp.int32, (1, LANES), 1) // 32
     zz, zy, yy, ay = [jnp.sum(jnp.where(lanes == n, row, 0.0), axis=1, keepdims=True) for n in range(4)]
@@ -508,23 +521,43 @@
     along = jnp.broadcast_to(alpha0 + alpha1 * (turn + growth), (8, LANES))
     across = jnp.broadcast_to(alpha1 * alpha0, (8, LANES))
 
-    def finish(q, carry):
-        for n in range(8):
-            s = 8 * q + n
-            for c in range(2):
-                to = pl.ds(64 * q + n, 8, stride=8)
-                z, u = Z[c, tile(s + PRED), :], U[c, tile(s + PRED), :]
-                out_x[c, to, :] = X[c, tile(s + PRED), :] + (along * z + across * u)
-                out_r[c, to, :] = R[c, tile(s), :] - (along * W[c, tile(s), :] + across * V[c, tile(s), :])
-        return carry
-
-    lax.fori_loop(0, groups, finish, 0)
+    factors[0] = along
+    factors[1] = across
 
     for t in range(3):
         sent(row_copies(t) + section_copies(t))
     sent((bits_copy, cross_copy))
     for copy in pending:
         copy.wait_send()
+
+
+def finish(X, Z, U, R, W, V, factors, solved, left_over, XO, RO, sem):
+    groups = XO.shape[1] // 64
+    along, across = factors[0], factors[1]
+    copies = []
+    for part in range(PARTS):
+        first, last = groups * part // PARTS, groups * (part + 1) // PARTS
+        for n, (out, to) in enumerate(((XO, solved), (RO, left_over))):
+
+            def group(q, carry):
+                for i in range(8):
+                    for c in range(2):
+                        here = pl.ds(pl.multiple_of(64 * q + 8 * i, 8), 8)
+                        held = pl.ds(pl.multiple_of(64 * q + 8 * (i + PRED), 8), 8)
+                        if n == 0:
+                            value = X[c, held, :] + (along * Z[c, held, :] + across * U[c, held, :])
+                        else:
+                            value = R[c, here, :] - (along * W[c, here, :] + across * V[c, here, :])
+                        out[c, pl.ds(64 * q + i, 8, stride=8), :] = value
+                return carry
+
+            lax.fori_loop(first, last, group, 0)
+            rows = pl.ds(64 * first, 64 * (last - first))
+            copy = pltpu.make_async_copy(out.at[:, rows], to.at[:, rows], sem.at[2 * part + n])
+            copy.start()
+            copies.append(copy)
+    for copy in copies:
+        copy.wait()
 
 
 def tiles(shard):
@@ -551,8 +584,7 @@
         f32((2, own, LANES)),
         f32((2, own, LANES)),
         pltpu.VMEM((own, LANES), jnp.int32),
-        *[f32((2, held, LANES)) for _ in range(3)],
-        *[f32((2, own, LANES)) for _ in range(5)],
+        *[f32((2, own, LANES)) for _ in range(2)],
         f32((3, own, LANES)),
         f32((6, own, LANES)),
         f32((PRED, own + 8 * PRED, LANES)),
@@ -574,18 +606,29 @@
         pltpu.SemaphoreType.DMA((len(stages),)),
         pltpu.SemaphoreType.REGULAR((3,)),
     ]
+    kept = [(2, held, LANES)] * 3 + [(2, own, LANES)] * 3 + [(2, 8, LANES)]
+    arguments = (tiles(forces), tiles(start), tiles(spring_bits), plane_stiffness, cross_weight, anchors)
+    parts = pl.pallas_call(
+        functools.partial(kernel, n_gz, n_rows, anchors.shape[0], stages),
+        out_shape=[pltpu.VMEM(shape, jnp.float32) for shape in kept],
+        in_specs=[pl.BlockSpec(memory_space=pltpu.HBM)] * 6,
+        out_specs=[pl.BlockSpec(memory_space=pltpu.VMEM)] * 7,
+        scratch_shapes=scratch,
+        compiler_params=pltpu.CompilerParams(
+            collective_id=0, has_side_effects=True, vmem_limit_bytes=24 * 1024 * 1024
+        ),
+        name="cg",
+    )(*[pltpu.with_memory_space_constraint(a, pltpu.HBM) for a in arguments])
     shape = jax.ShapeDtypeStruct((2, own, LANES), jnp.float32)
     solved, left_over = pl.pallas_call(
-        functools.partial(kernel, n_gz, n_rows, anchors.shape[0], stages),
-        out_shape=(pltpu.VMEM(shape.shape, jnp.float32),) * 2,
-        in_specs=[pl.BlockSpec(memory_space=pltpu.HBM)] * 6,
-        out_specs=[pl.BlockSpec(memory_space=pltpu.VMEM)] * 2,
-        scratch_shapes=scratch,
-        compiler_params=pltpu.CompilerParams(
-            collective_id=0, has_side_effects=True
-        ),
-        name="cg",
-    )(tiles(forces), tiles(start), tiles(spring_bits), plane_stiffness, cross_weight, anchors)
+        finish,
+        out_shape=(shape, shape),
+        in_specs=[pl.BlockSpec(memory_space=pltpu.VMEM)] * 7,
+        out_specs=[pl.BlockSpec(memory_space=pltpu.HBM)] * 2,
+        scratch_shapes=[f32((2, own, LANES)), f32((2, own, LANES)), pltpu.SemaphoreType.DMA((2 * PARTS,))],
+        compiler_params=pltpu.CompilerParams(vmem_limit_bytes=8 * 1024 * 1024),
+        name="finish",
+    )(*parts)
     return untiled(solved, sections, nodes), untiled(left_over, sections, nodes)
 
 

time: 32.7 us -> 30.3 us (0.927)
  local copies, waits for them, and re-layouts: 1.76 us -> 0 us
  Pallas kernels: 30.1 us -> 29.5 us
    pallas_call x1, Pallas kernels: 30.1 us -> 28.3 us  [per_device(): pl.pallas_call(functools.partial(kernel, n_gz, n_rows, anchors.shape[0],...]
    unnamed x2 -> x0, local copies, waits for them, and re-layouts: 1.76 us -> none
    pallas_call x0 -> x1, Pallas kernels: none -> 1.26 us  [per_device(): pl.pallas_call(finish, out_shape=(shape, shape), in_specs=[pl.BlockSpec(m...]
where the time goes in v4:
time: 30.3 us; the launch traced here: 30.2 us
  Pallas kernels  29.5 us (97%)
  between operations  0.64 us (2%)
    pallas_call x1, Pallas kernels, per_device(): pl.pallas_call(functools.partial(kernel, n_gz, n_rows, anchors.shape[0],...  28.3 us
    pallas_call x1, Pallas kernels, per_device(): pl.pallas_call(finish, out_shape=(shape, shape), in_specs=[pl.BlockSpec(m...  1.26 us

profile of v4, /device:TPU:1, one launch (start us, length us, event | category | flops | bytes accessed | tf_op | source)
XLA Modules:
  0.0 30.2 jit_solution(16667624766830976582)
XLA Ops:
  0.6 28.3 %cg.1 = (f32[2,816,128]{2,1,0:T(8,128)S(1)}, f32[2,816,128]{2,1,0:T(8,128)S(1)}, f32[2,816,128]{2,1,0:T(8,128)S(1)}, f32[2,768,128]{2,1,0:T(8,128)S(1)}, f32[2,7...) custom-call(f32[2,768,128]{2,1,0:T(8,128)} %bitcast.25, f32[2,768,128]{2,1,0:T(8,128)} %bitcast.26, ...), custom_call_target="tpu_custom_call" | custom-call | tf_op jit(solution)/shard_map/cg/pallas_call | solution.py:611
  28.9 1.3 %finish.1 = (f32[2,768,128]{2,1,0:T(8,128)}, f32[2,768,128]{2,1,0:T(8,128)}) custom-call(f32[2,816,128]{2,1,0:T(8,128)S(1)} %get-tuple-element.11.X, f32[2,816,128]{2,1,0:T(8,128)S(1)} %get-tuple-element.12.Z, f32[2,816,128]{2,1,0:T(8,128)S(1)} %get-tuple-element.13.U, f32[2,768,128]{2,1,0:T(8,128)S(1)} %get-tuple-element.14.R, ...), custom_call_target="tpu_custom_call" | custom-call | tf_op jit(solution)/shard_map/finish/pallas_call | solution.py:623

commit v5 on v4

--- a/solution.py
+++ b/solution.py
@@ -10,9 +10,8 @@
 GRID = 64
 PRED = 3
 LANES = 128
-PARTS = 3
+PARTS = 6
 APPLY_UNROLL = 18
-FILL_UNROLL = 18
 MESH = pl.DeviceIdType.MESH
 
 damping = 0.05
@@ -36,11 +35,11 @@
 
 def kernel(
     n_gz, n_rows, n_anchors, stages,
-    f_hbm, x_hbm, b_hbm, stiff_hbm, cross_hbm, anchors_hbm,
+    f_hbm, x_hbm, b_hbm, xtile_hbm, btile_hbm, stiff_hbm, cross_hbm, anchors_hbm,
     X, Z, U, R, W, V, factors,
     stiff, cross, anchors,
-    XS, FS, BS, Y, INV, DG, WP, K, TE, KS,
-    PS, HT, HB, BO, BT, PW, PI, PY, PH, PF, FX, *rest,
+    XS, FS, BS, XE, BE, Y, INV, DG, WP, K, TE, KS,
+    PS, HT, HB, BO, BT, PW, PI, PY, PH, PF, FX, FH, QS, HQ, HI, *rest,
 ):
     n_stages = len(stages)
     totals_out, totals_in = rest[:n_stages], rest[n_stages : 2 * n_stages]
@@ -52,15 +51,40 @@
     prev, nxt = {"gz": g - 1, "rows": r}, {"gz": g + 1, "rows": r}
     above, below = {"gz": g, "rows": r - 1}, {"gz": g, "rows": r + 1}
 
+    barrier = pltpu.get_barrier_semaphore()
+
+    def signal(sem, links):
+        for here, device in links:
+            pl.when(here)(functools.partial(pl.semaphore_signal, sem, 1, device_id=device, device_id_type=MESH))
+
+    def count(links):
+        return sum(jnp.where(here, 1, 0) for here, _ in links)
+
+    beside = ((has_prev, prev), (has_next, nxt))
+    signal(barrier, beside)
+    own = 8 * sections
+    head, body, foot = pl.ds(0, 64), pl.ds(64, own - 128), pl.ds(own - 64, 64)
     loads = [
         pltpu.make_async_copy(src, dst, load_sem.at[i])
         for i, (src, dst) in enumerate(
-            [(anchors_hbm, anchors), (stiff_hbm, stiff), (cross_hbm, cross), (b_hbm, BS), (x_hbm, XS), (f_hbm, FS)]
+            [
+                (stiff_hbm, stiff),
+                (cross_hbm, cross),
+                (b_hbm.at[head], BS.at[head]),
+                (btile_hbm.at[:, 7], BE),
+                (xtile_hbm.at[:, :, 0], XE.at[0]),
+                (xtile_hbm.at[:, :, 7], XE.at[1]),
+                (x_hbm.at[:, head], XS.at[:, head]),
+                (x_hbm.at[:, foot], XS.at[:, foot]),
+                (anchors_hbm, anchors),
+                (b_hbm.at[foot], BS.at[foot]),
+            ]
+            + ([(b_hbm.at[body], BS.at[body]), (x_hbm.at[:, body], XS.at[:, body])] if sections > 16 else [])
+            + [(f_hbm, FS)]
         )
     ]
-    for load in loads[:5]:
+    for load in loads[:-1]:
         load.start()
-
     ny, nz, nc = digit_sizes(n_gz)
     my_digits = (g // (nz * nc), (g // nc) & (nz - 1), g & (nc - 1), r)
 
@@ -68,31 +92,35 @@
         y, z, c, x = [(d + o) & (n - 1) for d, o, n in zip(my_digits, offset, (ny, nz, nc, n_rows))]
         return {"gz": (y * nz + z) * nc + c, "rows": x}
 
-    def steps(size, by):
-        return sorted({step % size for step in by} - {0})
-
-    beside = [(y, 0, 0, 0) for y in steps(ny, (1, -1))] + [(0, 0, 0, x) for x in steps(n_rows, (1, -1))]
-    beside += [(0, z, 0, 0) for z in steps(nz, (1, -1, 2, -2))]
-    word = (beside, [(0, 0, 0, x) for x in range(1, n_rows)], [(y, 0, 0, 0) for y in range(1, ny)])
+    def along_lines(by, axes="xyz"):
+        links = []
+        for axis, size, at in (("x", n_rows, r), ("y", ny, my_digits[0]), ("z", nz, my_digits[1])):
+            step = {"x": 0, "y": nz * nc, "z": nc}[axis] * by
+            if size > by and axis in axes:
+                move = by if axis == "x" else 0
+                links.append((at >= by, {"gz": g - step, "rows": r - move}))
+                links.append((at < size - by, {"gz": g + step, "rows": r + move}))
+        return links
+
+    lines = along_lines(1)
+    signal(barrier, lines)
+    word = (
+        lines,
+        along_lines(2),
+        along_lines(4, "z"),
+        [(None, member((0, 0, 0, x))) for x in range(1, n_rows)],
+        [(None, member((y, 0, 0, 0))) for y in range(1, ny)],
+    )
 
     def say(t):
-        for offset in word[t]:
-            pl.semaphore_signal(word_sem.at[t], inc=1, device_id=member(offset), device_id_type=MESH)
+        for here, device in word[t]:
+            tell = functools.partial(pl.semaphore_signal, word_sem.at[t], 1, device_id=device, device_id_type=MESH)
+            tell() if here is None else pl.when(here)(tell)
 
     def hear(t):
         if word[t]:
-            pl.semaphore_wait(word_sem.at[t], len(word[t]))
-
-    barrier = pltpu.get_barrier_semaphore()
-    for here, device in ((has_prev, prev), (has_next, nxt), (has_above, above), (has_below, below)):
-
-        @pl.when(here)
-        def _():
-            pl.semaphore_signal(barrier, inc=1, device_id=device, device_id_type=MESH)
-
-    greeted = stages[0] + beside
-    for offset in greeted:
-        pl.semaphore_signal(barrier, inc=1, device_id=member(offset), device_id_type=MESH)
+            told = len(word[t]) if word[t][0][0] is None else count(word[t])
+            pl.semaphore_wait(word_sem.at[t], told)
 
     lane = lax.broadcasted_iota(jnp.int32, (8, LANES), 1)
     sub = lax.broadcasted_iota(jnp.int32, (8, LANES), 0)
@@ -132,27 +160,13 @@
 
     base = g * sections
 
-    loads[0].wait()
-
-    def anchor_step(i, hits):
-        for n in range(8):
-            a = anchors[8 * i + n] - base
-            hits = tuple(jnp.where(sub == a - 8 * q, 1, hit) for q, hit in enumerate(hits))
-        return hits
-
-    hits = lax.fori_loop(0, n_anchors // 8, anchor_step, tuple(jnp.zeros((8, LANES), jnp.int32) for _ in range(groups)))
-    for q in range(groups):
-        TE[8 * q : 8 * q + 8, :] = jnp.where(hits[q] > 0, damping + anchor_stiffness, damping).astype(jnp.float32)
-
-    def cross_weights(s):
-        bits = BS[raw(s), :]
+    def cross_weights(s, bits):
+        for j in range(PRED):
+            kj = jnp.where(base + s > j, cross[j, s], 0.0) if isinstance(s, int) and s < PRED else cross[j, s]
+            K[j, tile(s), :] = jnp.where((bits & (8 << j)) != 0, jnp.full((8, LANES), kj, jnp.float32), zero)
+
+    def plane_weights(s, bits):
         KS[pl.ds(s, 1), :] = jnp.full((1, LANES), stiff[s], jnp.float32)
-        for j in range(PRED):
-            kj = jnp.where(base + s > j, cross[j, s], 0.0)
-            K[j, tile(s), :] = jnp.where((bits & (8 << j)) != 0, jnp.full((8, LANES), kj, jnp.float32), zero)
-        return bits
-
-    def plane_weights(s, bits):
         k = jnp.full((8, LANES), stiff[s], jnp.float32)
         wr = jnp.where((bits & mask_right) != 0, k, zero)
         wd = jnp.where((bits & mask_down) != 0, k, zero)
@@ -160,27 +174,23 @@
         for n, w in enumerate((wr, right(wr), wd, lowered(wd, GRID), wg, lowered(wg, GRID + 1))):
             WP[n, tile(s), :] = w
 
-    for load in loads[1:4]:
+    for load in loads[:8]:
         load.wait()
     for s in range(PRED):
-        cross_weights(s)
+        cross_weights(s, BS[raw(s), :])
 
     for q in range(groups // 2):
-        a = BS[64 * q + 56 : 64 * q + 64, :]
-        b = BS[64 * (q + groups // 2) + 56 : 64 * (q + groups // 2) + 64, :]
-        BO[8 * q : 8 * q + 8, :] = jnp.where(lo, half(a), b)
-
-    loads[4].wait()
+        BO[8 * q : 8 * q + 8, :] = jnp.where(lo, half(BE[q]), BE[q + groups // 2])
+
     for c in range(2):
         for s in list(range(PRED)) + list(range(sections - PRED, sections)):
             X[c, 8 * (s + PRED) : 8 * (s + PRED) + 8, :] = XS[c, pl.ds((s // 8) * 64 + s % 8, 8, stride=8), :]
     for q in range(groups):
         rows = slice(8 * q, 8 * q + 8)
-        PS[0, 0, rows, :] = pack_first(XS[0, 64 * q : 64 * q + 8, :], XS[1, 64 * q : 64 * q + 8, :])
-        PS[0, 1, rows, :] = pack_last(XS[0, 64 * q + 56 : 64 * q + 64, :], XS[1, 64 * q + 56 : 64 * q + 64, :])
-
-    near = sum(jnp.where(here, 1, 0) for here in (has_prev, has_next, has_above, has_below))
-    pl.semaphore_wait(barrier, near + len(greeted))
+        PS[0, 0, rows, :] = pack_first(XE[0, 0, q], XE[0, 1, q])
+        PS[0, 1, rows, :] = pack_last(XE[1, 0, q], XE[1, 1, q])
+
+    pl.semaphore_wait(barrier, count(beside) + count(lines))
 
     def remote(src, dst, at, device):
         return pltpu.make_async_remote_copy(
@@ -189,7 +199,6 @@
         )
 
     edge = 8 * PRED
-    own = 8 * sections
 
     def row_copies(t):
         return (
@@ -204,6 +213,16 @@
             (has_prev, has_next, remote(v.at[:, pl.ds(edge, edge)], v.at[:, pl.ds(own + edge, edge)], 4 * t + 3, prev)),
         )
 
+    def both_ways(part, src, to, at):
+        return (
+            (has_below, has_above, remote(src.at[1, part], to.at[0, part], at, below)),
+            (has_above, has_below, remote(src.at[0, part], to.at[1, part], at + 1, above)),
+        )
+
+    inverse_copies = both_ways(pl.ds(0, sections), PI, HI, 14)
+    middle_copies = both_ways(pl.ds(8, sections - 16), QS, HQ, 8) if sections > 16 else ()
+    outer_copies = both_ways(pl.ds(0, 8), QS, HQ, 16) + both_ways(pl.ds(sections - 8, 8), QS, HQ, 18)
+
     bits_copy = (has_below, has_above, remote(BO, BT, 12, below))
     cross_copy = (has_prev, has_next, remote(K.at[:, pl.ds(0, edge)], K.at[:, pl.ds(own, edge)], 13, prev))
 
@@ -220,8 +239,21 @@
             pl.when(sends)(copy.wait_send)
 
     start(row_copies(0) + section_copies(0) + (cross_copy, bits_copy))
-    loads[5].start()
+    loads[-1].start()
     say(0)
+
+    for load in loads[8:-1]:
+        load.wait()
+
+    def anchor_step(i, hits):
+        for n in range(8):
+            a = anchors[8 * i + n] - base
+            hits = tuple(jnp.where(sub == a - 8 * q, 1, hit) for q, hit in enumerate(hits))
+        return hits
+
+    hits = lax.fori_loop(0, n_anchors // 8, anchor_step, tuple(jnp.zeros((8, LANES), jnp.int32) for _ in range(groups)))
+    for q in range(groups):
+        TE[8 * q : 8 * q + 8, :] = jnp.where(hits[q] > 0, damping + anchor_stiffness, damping).astype(jnp.float32)
 
     wide = jnp.zeros((2, edge, LANES), jnp.float32)
 
@@ -239,11 +271,15 @@
     @pl.when(jnp.logical_not(has_above))
     def _():
         HT[...] = jnp.zeros(HT.shape, jnp.float32)
+        HI[0] = jnp.zeros(HI.shape[1:], jnp.float32)
+        HQ[0] = jnp.zeros(HQ.shape[1:], jnp.float32)
         BT[...] = jnp.zeros(BT.shape, jnp.int32)
 
     @pl.when(jnp.logical_not(has_below))
     def _():
         HB[...] = jnp.zeros(HB.shape, jnp.float32)
+        HI[1] = jnp.zeros(HI.shape[1:], jnp.float32)
+        HQ[1] = jnp.zeros(HQ.shape[1:], jnp.float32)
 
     ends = list(range(PRED)) + list(range(sections - PRED, sections))
     inner = sections - 2 * PRED
@@ -258,17 +294,24 @@
 
         return lax.fori_loop(0, inner // unroll, step, carry)
 
-    def fill(s, carry):
-        plane_weights(s, cross_weights(s))
-        for c in range(2):
-            X[c, tile(s + PRED), :] = XS[c, raw(s), :]
+    def fill(q, carry):
+        for i in range(8):
+            s = 8 * q + i
+            bits = BS[pl.ds(64 * q + i, 8, stride=8), :]
+            plane_weights(s, bits)
+            if not isinstance(s, int) or s >= PRED:
+                cross_weights(s, bits)
+            if not isinstance(s, int) or s not in ends:
+                for c in range(2):
+                    X[c, tile(s + PRED), :] = XS[c, pl.ds(64 * q + i, 8, stride=8), :]
         return carry
 
-    over_inner(fill, 0, FILL_UNROLL)
-    for s in range(PRED):
-        plane_weights(s, BS[raw(s), :])
-    for s in range(sections - PRED, sections):
-        plane_weights(s, cross_weights(s))
+    def fill_pair(p, carry):
+        return fill(2 * p + 2, fill(2 * p + 1, carry))
+
+    lax.fori_loop(0, (groups - 2) // 2, fill_pair, 0)
+    fill(0, 0)
+    fill(groups - 1, 0)
 
     def apply(v, out, s, first=False):
         wr, wl, wd, wu, wg, wv = [WP[n, tile(s), :] for n in range(6)]
@@ -336,11 +379,13 @@
 
     for q in range(groups):
         rows = rows_of(q)
-        bits = BS[64 * q + 56 : 64 * q + 64, :]
+        bits = BE[q]
         bits = jnp.where(lo, half(bits), bits)
         k = jnp.where(has_below, KS[rows, :], zero)
         PW[2, rows, :] = jnp.where((bits & 2) != 0, k, zero) * down_scale
-        PW[3, rows, :] = jnp.where(((bits & 4) != 0) & open_column, k, zero)
+        slant_weight = jnp.where(((bits & 4) != 0) & open_column, k, zero)
+        PW[3, rows, :] = slant_weight
+        PW[5, rows, :] = right(slant_weight)
 
     middle = range(1, groups - 1)
     outer = sorted({0, groups - 1})
@@ -352,18 +397,28 @@
                 PY[n, rows, :] = part
                 PH[n, rows, :] = half(PS[t, n, rows, :])
 
+    def pull_up(mine, turned, other, down, slant_shifted):
+        slant = 0.625 * (right(other) - mine) + 0.375 * (pltpu.roll(other, GRID + 1, 1) - turned)
+        return down * (mine - other) - slant_shifted * slant
+
+    def pull_down(mine, turned, other, down, slant_weight):
+        slant = 0.625 * (mine - left(other)) + 0.375 * (turned - pltpu.roll(other, GRID - 1, 1))
+        return down * (mine - other) + slant_weight * slant
+
     def outside(t, q):
         rows = rows_of(q)
-        mine, turned, other = PS[t, 0, rows, :], PH[0, rows, :], HT[t, rows, :]
-        slant = 0.625 * (right(other) - mine) + 0.375 * (pltpu.roll(other, GRID + 1, 1) - turned)
-        top = PW[0, rows, :] * (mine - other) - PW[1, rows, :] * slant
-        mine, turned, other = PS[t, 1, rows, :], PH[1, rows, :], HB[t, rows, :]
-        slant = 0.625 * (mine - left(other)) + 0.375 * (turned - pltpu.roll(other, GRID - 1, 1))
-        bottom = PW[2, rows, :] * (mine - other) + PW[3, rows, :] * slant
+        top = pull_up(PS[t, 0, rows, :], PH[0, rows, :], HT[t, rows, :], PW[0, rows, :], PW[1, rows, :])
+        bottom = pull_down(PS[t, 1, rows, :], PH[1, rows, :], HB[t, rows, :], PW[2, rows, :], PW[3, rows, :])
         FX[0, rows, :] = top
         FX[1, rows, :] = bottom
         return top, bottom
 
+    def outside_there(t, q):
+        rows = rows_of(q)
+        above_row, below_row = HT[t, rows, :], HB[t, rows, :]
+        FH[0, rows, :] = pull_down(above_row, half(above_row), PS[t, 0, rows, :], PW[0, rows, :], PW[4, rows, :])
+        FH[1, rows, :] = pull_up(below_row, half(below_row), PS[t, 1, rows, :], PW[2, rows, :], PW[5, rows, :])
+
     def add(old, new):
         return old + new
 
@@ -371,22 +426,25 @@
         return new
 
     before_rows(0, Y, middle)
-    loads[5].wait()
+    loads[-1].wait()
     for q in range(groups):
         rows = rows_of(q)
         head, foot = slice(64 * q, 64 * q + 8), slice(64 * q + 56, 64 * q + 64)
         PF[0, rows, :] = pack_first(FS[0, head, :], FS[1, head, :])
         PF[1, rows, :] = pack_last(FS[0, foot, :], FS[1, foot, :])
 
+    hear(0)
+    say(1)
     arrive((cross_copy,) + section_copies(0) + row_copies(0) + (bits_copy,))
-    hear(0)
     for q in range(groups // 2):
         both = BT[rows_of(q), :]
         for n, bits in enumerate((jnp.where(lo, both, half(both)), jnp.where(lo, half(both), both))):
             rows = rows_of(q + n * (groups // 2))
             k = jnp.where(has_above, KS[rows, :], zero)
             PW[0, rows, :] = jnp.where((bits & 2) != 0, k, zero) * down_scale
-            PW[1, rows, :] = right(jnp.where(((bits & 4) != 0) & open_column, k, zero))
+            slant_weight = jnp.where(((bits & 4) != 0) & open_column, k, zero)
+            PW[1, rows, :] = right(slant_weight)
+            PW[4, rows, :] = slant_weight
 
     for s in ends:
         first_apply(s, 0)
@@ -402,13 +460,6 @@
             res = PF[n, rows, :] - (PY[n, rows, :] + part)
             PF[n, rows, :] = res
             PS[1, n, rows, :] = res * PI[n, rows, :]
-    start(row_copies(1))
-    say(1)
-    for q in range(groups):
-        rows = rows_of(q)
-        change_rows(Y, q, FX[0, rows, :], FX[1, rows, :], add)
-        change_rows(INV, q, PI[0, rows, :], PI[1, rows, :], put)
-
     def residual(s, total):
         for c in range(2):
             res = FS[c, raw(s), :] - Y[c, tile(s), :]
@@ -418,11 +469,22 @@
             total = total + res * pre
         return total
 
+    def change_first(q):
+        rows = rows_of(q)
+        change_rows(Y, q, FX[0, rows, :], FX[1, rows, :], add)
+        change_rows(INV, q, PI[0, rows, :], PI[1, rows, :], put)
+
+    for q in outer:
+        change_first(q)
     sum0 = zero
     for s in ends:
         sum0 = residual(s, sum0)
-    start(section_copies(1))
+    start(row_copies(1) + section_copies(1) + inverse_copies)
+    for q in middle:
+        change_first(q)
     sum0 = over_inner(residual, sum0, 10)
+    hear(1)
+    say(2)
 
     def second_apply(s, carry):
         apply(Z, W, s)
@@ -431,18 +493,28 @@
     over_inner(second_apply, 0, APPLY_UNROLL)
     before_rows(1, W, middle)
 
+    def send_part(some):
+        for q in some:
+            for n in range(2):
+                QS[n, rows_of(q), :] = PF[n, rows_of(q), :] - PY[n, rows_of(q), :]
+
+    send_part(middle)
+    start(middle_copies)
+
     arrive(section_copies(1) + row_copies(1))
-    hear(1)
     for s in ends:
         second_apply(s, 0)
     before_rows(1, W, outer)
-    for q in range(groups):
-        rows = rows_of(q)
-        for n, part in enumerate(outside(1, q)):
-            PS[2, n, rows, :] = (PF[n, rows, :] - (PY[n, rows, :] + part)) * PI[n, rows, :]
-    start(row_copies(2))
-    say(2)
-    for q in range(groups):
+    send_part(outer)
+    start(outer_copies)
+    def own_part(some):
+        for q in some:
+            rows = rows_of(q)
+            for n, part in enumerate(outside(1, q)):
+                PS[2, n, rows, :] = (QS[n, rows, :] - part) * PI[n, rows, :]
+
+    own_part(outer)
+    for q in outer:
         change_rows(W, q, FX[0, rows_of(q), :], FX[1, rows_of(q), :], add)
 
     def second(s, totals):
@@ -459,14 +531,26 @@
     for s in ends:
         sums = second(s, sums)
     start(section_copies(2))
+    own_part(middle)
+    for q in range(groups):
+        outside_there(1, q)
+    for q in middle:
+        change_rows(W, q, FX[0, rows_of(q), :], FX[1, rows_of(q), :], add)
     sum1, sum2 = over_inner(second, sums, 10)
+    hear(2)
+    say(3)
     sum3 = over_inner(lambda s, total: total + apply(U, V, s), zero, APPLY_UNROLL)
     for q in range(groups):
         for n in range(2):
             PH[n, rows_of(q), :] = half(PS[2, n, rows_of(q), :])
 
-    arrive(section_copies(2) + row_copies(2))
-    hear(2)
+    hear(3)
+    say(4)
+    arrive(section_copies(2) + inverse_copies + middle_copies + outer_copies)
+    for q in range(groups):
+        rows = rows_of(q)
+        HT[2, rows, :] = (HQ[0, rows, :] - FH[0, rows, :]) * HI[0, rows, :]
+        HB[2, rows, :] = (HQ[1, rows, :] - FH[1, rows, :]) * HI[1, rows, :]
     for s in ends:
         sum3 = sum3 + apply(U, V, s)
     for q in range(groups):
@@ -486,6 +570,8 @@
             change_rows(V, q, FX[0, rows_of(q), :], FX[1, rows_of(q), :], add)
 
     for t, group in enumerate(stages):
+        if t == 1:
+            hear(4)
         totals_out[t][0] = row
         for n, offset in enumerate(group):
             copy = pltpu.make_async_remote_copy(
@@ -502,8 +588,8 @@
             finish_rows()
         everyone.wait_recv()
         pending.append(everyone)
-        count = len(group)
-        cuts = [count * n // 6 for n in range(7)] if count > 30 else [0, count]
+        members = len(group)
+        cuts = [members * n // 6 for n in range(7)] if members > 30 else [0, members]
         parts = [jnp.sum(totals_in[t][a:b], axis=0) for a, b in zip(cuts, cuts[1:])]
         while len(parts) > 1:
             parts = [sum(parts[n : n + 2][1:], parts[n]) for n in range(0, len(parts), 2)]
@@ -525,8 +611,8 @@
     factors[1] = across
 
     for t in range(3):
-        sent(row_copies(t) + section_copies(t))
-    sent((bits_copy, cross_copy))
+        sent((row_copies(t) if t < 2 else ()) + section_copies(t))
+    sent((bits_copy, cross_copy) + inverse_copies + middle_copies + outer_copies)
     for copy in pending:
         copy.wait_send()
 
@@ -535,8 +621,9 @@
     groups = XO.shape[1] // 64
     along, across = factors[0], factors[1]
     copies = []
-    for part in range(PARTS):
-        first, last = groups * part // PARTS, groups * (part + 1) // PARTS
+    count = min(PARTS, groups)
+    for part in range(count):
+        first, last = groups * part // count, groups * (part + 1) // count
         for n, (out, to) in enumerate(((XO, solved), (RO, left_over))):
 
             def group(q, carry):
@@ -584,6 +671,8 @@
         f32((2, own, LANES)),
         f32((2, own, LANES)),
         pltpu.VMEM((own, LANES), jnp.int32),
+        f32((2, 2, sections // 8, 8, LANES)),
+        pltpu.VMEM((sections // 8, 8, LANES), jnp.int32),
         *[f32((2, own, LANES)) for _ in range(2)],
         f32((3, own, LANES)),
         f32((6, own, LANES)),
@@ -595,23 +684,25 @@
         f32((3, sections, LANES)),
         pltpu.VMEM((sections // 2, LANES), jnp.int32),
         pltpu.VMEM((sections // 2, LANES), jnp.int32),
-        f32((4, sections, LANES)),
-        *[f32((2, sections, LANES)) for _ in range(5)],
+        f32((6, sections, LANES)),
+        *[f32((2, sections, LANES)) for _ in range(9)],
         *[f32((1, 1, LANES)) for _ in stages],
         *[f32((len(group), 1, LANES)) for group in stages],
-        pltpu.SemaphoreType.DMA((6,)),
-        pltpu.SemaphoreType.DMA((14,)),
-        pltpu.SemaphoreType.DMA((14,)),
+        pltpu.SemaphoreType.DMA((13,)),
+        pltpu.SemaphoreType.DMA((20,)),
+        pltpu.SemaphoreType.DMA((20,)),
         pltpu.SemaphoreType.DMA((len(stages),)),
         pltpu.SemaphoreType.DMA((len(stages),)),
-        pltpu.SemaphoreType.REGULAR((3,)),
+        pltpu.SemaphoreType.REGULAR((5,)),
     ]
     kept = [(2, held, LANES)] * 3 + [(2, own, LANES)] * 3 + [(2, 8, LANES)]
-    arguments = (tiles(forces), tiles(start), tiles(spring_bits), plane_stiffness, cross_weight, anchors)
+    shaped = tiles(start), tiles(spring_bits)
+    split = [a.reshape(*a.shape[:-2], sections // 8, 8, 8, LANES) for a in shaped]
+    arguments = (tiles(forces), *shaped, *split, plane_stiffness, cross_weight, anchors)
     parts = pl.pallas_call(
         functools.partial(kernel, n_gz, n_rows, anchors.shape[0], stages),
         out_shape=[pltpu.VMEM(shape, jnp.float32) for shape in kept],
-        in_specs=[pl.BlockSpec(memory_space=pltpu.HBM)] * 6,
+        in_specs=[pl.BlockSpec(memory_space=pltpu.HBM)] * 8,
         out_specs=[pl.BlockSpec(memory_space=pltpu.VMEM)] * 7,
         scratch_shapes=scratch,
         compiler_params=pltpu.CompilerParams(

time: 30.3 us -> 29.8 us (0.983)
  Pallas kernels: 29.5 us -> 29.1 us
    pallas_call x1, Pallas kernels: 28.3 us -> 27.8 us  [per_device(): pl.pallas_call(functools.partial(kernel, n_gz, n_rows, anchors.shape[0],...]
where the time goes in v5:
time: 29.8 us; the launch traced here: 29.7 us
  Pallas kernels  29.1 us (98%)
  between operations  0.64 us (2%)
    pallas_call x1, Pallas kernels, per_device(): pl.pallas_call(functools.partial(kernel, n_gz, n_rows, anchors.shape[0],...  27.8 us
    pallas_call x1, Pallas kernels, per_device(): pl.pallas_call(finish, out_shape=(shape, shape), in_specs=[pl.BlockSpec(m...  1.27 us

profile of v5, /device:TPU:1, one launch (start us, length us, event | category | flops | bytes accessed | tf_op | source)
XLA Modules:
  0.0 29.7 jit_solution(12880885555335680922)
XLA Ops:
  0.6 27.8 %cg.1 = (f32[2,816,128]{2,1,0:T(8,128)S(1)}, f32[2,816,128]{2,1,0:T(8,128)S(1)}, f32[2,816,128]{2,1,0:T(8,128)S(1)}, f32[2,768,128]{2,1,0:T(8,128)S(1)}, f32[2,7...) custom-call(f32[2,768,128]{2,1,0:T(8,128)} %bitcast.29, f32[2,768,128]{2,1,0:T(8,128)} %bitcast.25, ...), custom_call_target="tpu_custom_call" | custom-call | tf_op jit(solution)/shard_map/cg/pallas_call | solution.py:702
  28.5 1.3 %finish.1 = (f32[2,768,128]{2,1,0:T(8,128)}, f32[2,768,128]{2,1,0:T(8,128)}) custom-call(f32[2,816,128]{2,1,0:T(8,128)S(1)} %get-tuple-element.11.X, f32[2,816,128]{2,1,0:T(8,128)S(1)} %get-tuple-element.12.Z, f32[2,816,128]{2,1,0:T(8,128)S(1)} %get-tuple-element.13.U, f32[2,768,128]{2,1,0:T(8,128)S(1)} %get-tuple-element.14.R, ...), custom_call_target="tpu_custom_call" | custom-call | tf_op jit(solution)/shard_map/finish/pallas_call | solution.py:714
